TPU v7x, 768 devices: a whole 4x8x12 slice. The times are simulated.
768 devices in a mesh: dp: 16 (over y, core), expert: 12 (over z), tensor: 4 (over x).
Axes of the slice: x: 4, y: 8, z: 12, core: 2. Of those that a mesh axis runs over, the one named last changes fastest.
Arguments:
- router_input: bfloat16 [24576, 2048], P(('dp', 'expert'), 'tensor'), may hold values from -6 to 6
- router_weight: bfloat16 [2048, 8], replicated, may hold values from -0.125 to 0.125
- expert_ids: int32 [24576, 2], P(('dp', 'expert', 'tensor')), may hold values from 0 to 7, all different within a row; in each aligned block of 32 rows (0 to 31, 32 to 63, ...) at most 9 rows name the same one
- down_weight: bfloat16 [61440, 2048], P(('expert', 'tensor')), may hold values from -0.0625 to 0.0625
- hidden: bfloat16 [16, 432, 61440], P('dp', None, ('expert', 'tensor')), may hold values from -6 to 6
- grad_output: bfloat16 [24576, 2048], P(('dp', 'expert', 'tensor')), may hold values from -4 to 4
Outputs:
- weight_grad: bfloat16 [61440, 2048], P(('expert', 'tensor', 'dp'))
- hidden_grad: bfloat16 [16, 432, 61440], P('dp', None, ('expert', 'tensor'))
- router_grad: float32 [2048, 8], replicated
- input_grad: bfloat16 [24576, 2048], P(('dp', 'expert', 'tensor'))
Inputs may be any that keep to these rules, and one draw needn't show every extreme that they name: `expert_ids`: each row names 2 different experts. Within the 32 rows of one device no expert is named more than 9 times, and some device's rows name some expert exactly 9 times.
All inputs are finite; a program needn't handle non-finite values.
Results may differ from a plain program's by a relative error of at most 0.018.
Values may be sent and summed in bfloat16 or wider, within the bound.
A program may use at most 64 MiB of HBM per device.

v0:
```python
import functools

import jax
import jax.numpy as jnp
from jax import lax
from jax.sharding import Mesh
from jax.sharding import PartitionSpec as P

DP = ("dp_0", "dp_1")
DP_EXPERT_TENSOR = ("dp_0", "dp_1", "expert", "tensor")
DP_EXPERT = ("dp_0", "dp_1", "expert")
EXPERT_TENSOR_DP = ("expert", "tensor", "dp_0", "dp_1")


def by_axis(array, axes):
    return functools.reduce(lax.psum, axes, array)


def per_device(router_input, router_weight, expert_ids, down_weight, hidden, grad_output):
    token_rows = grad_output.shape[0]
    model_width = grad_output.shape[1]
    expert_count = router_weight.shape[1]
    choose_count = expert_ids.shape[1]
    expert_ranks = lax.axis_size("expert")
    tensor_ranks = lax.axis_size("tensor")
    sources = expert_ranks * tensor_ranks
    spread = sources // expert_count
    capacity = hidden.shape[1] // sources
    full_input = lax.all_to_all(router_input, "tensor", split_axis=0, concat_axis=1, tiled=True)
    logits = jnp.dot(full_input, router_weight, preferred_element_type=jnp.float32)
    labels = jnp.arange(expert_count, dtype=jnp.int32)
    onehot_int = (expert_ids[:, :, None] == labels).astype(jnp.int32)
    onehot = onehot_int.astype(jnp.float32)
    picked = jnp.sum(onehot * logits[:, None, :], axis=2)
    first_gate = jax.nn.sigmoid(picked[:, 0] - picked[:, 1])
    second_gate = jax.nn.sigmoid(picked[:, 1] - picked[:, 0])
    gate_values = jnp.stack([first_gate, second_gate], axis=1)
    gate_low = gate_values.astype(jnp.bfloat16)
    flat_hits = onehot_int.reshape(token_rows * choose_count, expert_count)
    before = jnp.cumsum(flat_hits, axis=0) - flat_hits
    slot_pos = jnp.sum(before * flat_hits, axis=1).reshape(token_rows, choose_count)
    slot_ids = jnp.arange(capacity, dtype=jnp.int32)
    dispatch_table = onehot[:, :, :, None] * (slot_pos[:, :, None, None] == slot_ids).astype(
        jnp.float32
    )
    slot_table = jnp.sum(dispatch_table, axis=1).astype(jnp.bfloat16)
    packed_grad = jnp.einsum(
        "rec,rd->ecd", slot_table, grad_output, preferred_element_type=jnp.float32
    ).astype(jnp.bfloat16)
    packed_gate = jnp.einsum("rkec,rk->ec", dispatch_table, gate_low.astype(jnp.float32)).astype(
        jnp.bfloat16
    )
    send_grad = jnp.repeat(packed_grad, spread, axis=0)
    send_gate = jnp.repeat(packed_gate, spread, axis=0)
    recv_grad, recv_gate = (
        lax.all_to_all(send_grad, ("expert", "tensor"), split_axis=0, concat_axis=0, tiled=True),
        lax.all_to_all(send_gate, ("expert", "tensor"), split_axis=0, concat_axis=0, tiled=True),
    )
    recv_grad = recv_grad.reshape(sources * capacity, model_width)
    recv_gate = recv_gate.reshape(sources * capacity).astype(jnp.float32)
    hidden_rows = hidden[0]
    gated_grad = (recv_gate[:, None] * recv_grad.astype(jnp.float32)).astype(jnp.bfloat16)
    expert_image = lax.dot_general(
        recv_grad, down_weight, (((1,), (1,)), ((), ())), preferred_element_type=jnp.float32
    )
    hidden_part = (recv_gate[:, None] * expert_image).astype(jnp.bfloat16)
    gate_partial = jnp.sum(hidden_rows.astype(jnp.float32) * expert_image, axis=1).reshape(
        sources, capacity
    )
    returned = lax.all_to_all(
        gate_partial, ("expert", "tensor"), split_axis=0, concat_axis=0, tiled=True
    )
    expert_sums = jnp.sum(returned.reshape(expert_count, spread, capacity), axis=1)
    gate_grad = jnp.einsum("rkec,ec->rk", dispatch_table, expert_sums)
    mixed_term = jnp.sum(gate_values * gate_grad, axis=1, keepdims=True)
    logit_part = gate_values * (gate_grad - mixed_term)
    logit_grad = jnp.sum(onehot * logit_part[:, :, None], axis=1)
    input_grad = jnp.dot(
        logit_grad, router_weight.astype(jnp.float32).T, precision=lax.Precision.HIGHEST
    ).astype(jnp.bfloat16)
    router_local = jnp.dot(
        full_input.astype(jnp.float32).T, logit_grad, precision=lax.Precision.HIGHEST
    )
    router_grad = by_axis(router_local, DP_EXPERT_TENSOR)
    weight_sum = lax.psum_scatter(
        lax.dot_general(
            hidden_rows, gated_grad, (((0,), (0,)), ((), ())), preferred_element_type=jnp.float32
        ).astype(jnp.bfloat16),
        DP,
        scatter_dimension=0,
        tiled=True,
    )
    return (weight_sum, hidden_part[None], router_grad, input_grad)


def solution(mesh):
    finer = Mesh(
        mesh.devices.reshape(8, 2, mesh.shape["expert"], mesh.shape["tensor"]),
        ("dp_0", "dp_1", "expert", "tensor"),
    )
    placed = (
        P(DP_EXPERT, "tensor"),
        P(),
        P(DP_EXPERT_TENSOR, None),
        P(("expert", "tensor"), None),
        P(DP, None, ("expert", "tensor")),
        P(DP_EXPERT_TENSOR, None),
    )
    return jax.shard_map(
        per_device,
        mesh=finer,
        in_specs=placed,
        out_specs=(
            P(EXPERT_TENSOR_DP, None),
            P(DP, None, ("expert", "tensor")),
            P(),
            P(DP_EXPERT_TENSOR, None),
        ),
        check_vma=False,
    )
```

profile of v0, /device:TPU:1, one launch (start us, length us, event | category | flops | bytes accessed | tf_op | source)
XLA Modules:
  0.0 513.8 jit_solution(1472507924005066732)
XLA Ops:
  8.0 5.0 all-to-all-start
  13.0 0.7 convert_convert_fusion
  13.7 0.8 copy.31
  14.7 0.2 select_reduce_fusion
  15.1 2.7 all-to-all-done
  17.8 0.9 fusion.17
  18.7 0.7 multiply_reduce_fusion.3
  19.5 0.4 fusion.5
  20.3 0.7 copy.34
  21.0 16.2 %all-to-all-start.1 = ((bf16[48,1,9]{2,1,0:T(2,128)(2,1)}), bf16[48,1,9]{2,1,0:T(2,128)(2,1)S(1)}, u32[]{:S(2)}, u32[]{:S(2)}) async-start(bf16[48,1,9]{2,1,0:T(2,128)(2,1)} %copy.34), calls=%async_computation.1 | async-start | bytes 49152 | tf_op jit(solution)/shard_map/all_to_all | solution.py:57
  37.2 0.3 convolution_convert_fusion.1
  37.4 10.6 %all-to-all-done.1 = bf16[48,1,9]{2,1,0:T(2,128)(2,1)S(1)} async-done(((bf16[48,1,9]{2,1,0:T(2,128)(2,1)}), bf16[48,1,9]{2,1,0:T(2,128)(2,1)S(1)}, u32[]{:S(2)}, u32[]{:S(2)}) %all-to-all-start.1) | async-done | bytes 896 | tf_op jit(solution)/shard_map/all_to_all | solution.py:57
  48.0 2.1 broadcast_in_dim.7
  50.1 4.7 all-to-all-start.2
  55.1 100.5 %all-to-all-done.2 = bf16[48,9,2048]{2,1,0:T(8,128)(2,1)S(1)} async-done(((bf16[48,9,2048]{2,1,0:T(8,128)(2,1)}), bf16[48,9,2048]{2,1,0:T(8,128)(2,1)S(1)}, u32[]{:S(2)}, u32[]{:S(2)}) %all-to-all-start.2) | async-done | bytes 1769504 | tf_op jit(solution)/shard_map/all_to_all | solution.py:56
  155.6 2.2 reshape.69
  157.8 6.8 %multiply_reduce_fusion = (f32[432]{0:T(512)S(1)}, bf16[1,432,1280]{2,1,0:T(8,128)(2,1)}) fusion(bf16[1,432,1280]{2,1,0:T(8,128)(2,1)} %param.10, f32[432]{0:T(512)S(1)} %reshape.72, bf16[432,2048]{1,0:T(8,128)(2,1)} %reshape.69, bf16[1280,2048]{1,0:T(8,128)(2,1)} %param.9), kind=kOutput, calls=%fused_computation.6 | convolution fusion | flops 2267688448 | bytes 9227648 | tf_op jit(solution)/shard_map/dot_general | solution.py:63
  164.7 23.7 %all_to_all.42 = f32[48,1,9]{2,1,0:T(1,128)S(1)} all-to-all(f32[48,1,9]{2,1,0:T(1,128)S(1)} %bitcast.49), channel_id=1, replica_groups=mesh['dp_0'=8,'dp_1'=2,'expert'=12,'tensor'=4] {'expert','tensor'}, dimensions={0} | all-to-all | bytes 3456 | tf_op jit(solution)/shard_map/all_to_all | solution.py:70
  188.7 0.2 fusion.3
  188.9 0.8 convolution_bitcast_fusion
  189.8 74.9 %all-reduce.5.cloned.1.call-done = f32[2048,8]{0,1:T(8,128)} async-done(((f32[2048,8]{0,1:T(8,128)}), f32[2048,8]{0,1:T(8,128)}) %all-reduce.5.cloned.1.call-update) | async-done | bytes 65552 | tf_op jit(solution)/shard_map/psum | solution.py:16
  264.8 47.7 %all-reduce.7.cloned.1.call-done = f32[2048,8]{0,1:T(8,128)} async-done(((f32[2048,8]{0,1:T(8,128)}), f32[2048,8]{0,1:T(8,128)}) %all-reduce.7.cloned.1.call-update) | async-done | bytes 65552 | tf_op jit(solution)/shard_map/psum | solution.py:16
  312.6 2.2 multiply_convert_fusion
  314.8 3.1 convert_element_type.93
  317.9 100.7 %all-reduce.9.cloned.1.call-done = f32[2048,8]{0,1:T(8,128)} async-done(((f32[2048,8]{0,1:T(8,128)}), f32[2048,8]{0,1:T(8,128)}) %all-reduce.9.cloned.1.call-update) | async-done | bytes 65552 | tf_op jit(solution)/shard_map/psum | solution.py:16
  418.7 4.7 fusion
  423.4 7.9 %copy.43 = bf16[1280,2048]{1,0:T(8,128)(2,1)} copy(bf16[1280,2048]{0,1:T(8,128)(2,1)} %fusion) | data formatting | bytes 10485760
  431.4 0.7 copy-done.1
  432.1 1.0 convolution_convert_fusion.2
  433.1 48.1 %all-reduce.11.cloned.1.call-done = f32[2048,8]{0,1:T(8,128)} async-done(((f32[2048,8]{0,1:T(8,128)}), f32[2048,8]{0,1:T(8,128)}) %all-reduce.11.cloned.1.call-update) | async-done | bytes 65552 | tf_op jit(solution)/shard_map/psum | solution.py:16
  481.1 24.1 %reduce-scatter.4.cloned.1.call-done = bf16[80,2048]{1,0:T(8,128)(2,1)} async-done(((bf16[1280,2048]{1,0:T(8,128)(2,1)}), bf16[80,2048]{1,0:T(8,128)(2,1)}) %reduce-scatter.4.cloned.1.call-update) | async-done | bytes 327696
  505.2 1.5 copy.56
  (40 shorter events, 1.8 us)
Async XLA Ops:
  8.0 29.2 %copy-start = (bf16[32,2048]{1,0:T(8,128)(2,1)S(1)}, bf16[32,2048]{1,0:T(8,128)(2,1)}, u32[]{:S(2)}) copy-start(bf16[32,2048]{1,0:T(8,128)(2,1)} %param.11) | copy-start | bytes 393220
  8.0 9.8 %all-to-all-start = ((bf16[4,32,512]{2,1,0:T(8,128)(2,1)}), bf16[4,32,512]{2,1,0:T(8,128)(2,1)S(1)}, u32[]{:S(2)}, u32[]{:S(2)}) async-start(bf16[4,32,512]{2,1,0:T(8,128)(2,1)} %bitcast.47), calls=%async_computation | async-start | bytes 262144 | tf_op jit(solution)/shard_map/all_to_all | solution.py:29
  21.0 27.0 %all-to-all-start.1 = ((bf16[48,1,9]{2,1,0:T(2,128)(2,1)}), bf16[48,1,9]{2,1,0:T(2,128)(2,1)S(1)}, u32[]{:S(2)}, u32[]{:S(2)}) async-start(bf16[48,1,9]{2,1,0:T(2,128)(2,1)} %copy.34), calls=%async_computation.1 | async-start | bytes 49152 | tf_op jit(solution)/shard_map/all_to_all | solution.py:57
  50.1 105.5 %all-to-all-start.2 = ((bf16[48,9,2048]{2,1,0:T(8,128)(2,1)}), bf16[48,9,2048]{2,1,0:T(8,128)(2,1)S(1)}, u32[]{:S(2)}, u32[]{:S(2)}) async-start(bf16[48,9,2048]{2,1,0:T(8,128)(2,1)} %bitcast.43), calls=%async_computation.2 | async-start | bytes 6291456 | tf_op jit(solution)/shard_map/all_to_all | solution.py:56
  54.8 209.9 %all-reduce.5.cloned.1.call-start = ((), (), s32[]{:S(2)}) async-start(), calls=%async_computation.5 | async-start | bytes 131072 | tf_op jit(solution)/shard_map/psum | solution.py:16
  157.8 31.1 %copy-start.2 = (s32[32,2]{0,1:T(2,128)S(1)}, s32[32,2]{0,1:T(2,128)}, u32[]{:S(2)}) copy-start(s32[32,2]{0,1:T(2,128)} %param.8) | copy-start | bytes 772
  189.8 122.8 %all-reduce.7.cloned.1.call-start = ((), (), s32[]{:S(2)}) async-start(), calls=%async_computation.6 | async-start | bytes 131072 | tf_op jit(solution)/shard_map/psum | solution.py:16
  264.7 153.9 %all-reduce.9.cloned.1.call-start = ((), (), s32[]{:S(2)}) async-start(), calls=%async_computation.7 | async-start | bytes 131072 | tf_op jit(solution)/shard_map/psum | solution.py:16
  312.5 168.6 %all-reduce.11.cloned.1.call-start = ((), (), s32[]{:S(2)}) async-start(), calls=%async_computation.8 | async-start | bytes 131072 | tf_op jit(solution)/shard_map/psum | solution.py:16
  314.8 103.9 %copy-start.3 = (bf16[1,432,1280]{2,1,0:T(8,128)(2,1)S(1)}, bf16[1,432,1280]{2,1,0:T(8,128)(2,1)}, u32[]{:S(2)}) copy-start(bf16[1,432,1280]{2,1,0:T(8,128)(2,1)} %param.10) | copy-start | bytes 3317764
  418.6 86.6 %reduce-scatter.4.cloned.1.call-start = ((), (), s32[]{:S(2)}) async-start(), calls=%async_computation.9 | async-start | bytes 5570560
  431.3 0.8 copy-start.1
Sparse Core Ops, SparseCore 0:
  189.9 74.7 all-reduce.4
  267.8 44.6 all-reduce.6
  314.9 103.7 all-reduce.8
  420.8 60.3 all-reduce.10
Sparse Core Ops, SparseCore 1:
  431.4 73.7 reduce-scatter.3
where the time goes:
time: 515 us; the launch traced here: 514 us
  waiting for transfers between devices  409 us (79%)
  starting transfers between devices  26 us (5%)
  blocking collectives  23.7 us (5%)
  local copies, waits for them, and re-layouts  20 us (4%)
  between operations  15.4 us (3%)
  matrix products  15.1 us (3%)
    psum x4, waiting for transfers between devices, by_axis(): return functools.reduce(lax.psum, axes, array)  271 us
    all_to_all x1, waiting for transfers between devices, per_device(): lax.all_to_all(send_grad, ('expert', 'tensor'), split_axis=0, concat_axis...  101 us
    unnamed x6, waiting for transfers between devices  24.1 us
    all_to_all x1, blocking collectives, per_device(): lax.all_to_all(gate_partial, ('expert', 'tensor'), split_axis=0, concat_a...  23.7 us
    all_to_all x1, starting transfers between devices, per_device(): lax.all_to_all(send_gate, ('expert', 'tensor'), split_axis=0, concat_axis...  16.2 us
    unnamed x11, local copies, waits for them, and re-layouts  10.9 us
    all_to_all x1, waiting for transfers between devices, per_device(): lax.all_to_all(send_gate, ('expert', 'tensor'), split_axis=0, concat_axis...  10.6 us
  transfers between devices with their start and end apart: 8, of which 8 were waited for; matrix products, arithmetic and copies ran while one was open for 4% of the time, Pallas kernels for 0%

commit v1 on v0

v1 whole, which is shorter than its diff:
```python
import functools

import jax
import jax.numpy as jnp
from jax import lax
from jax.experimental import pallas as pl
from jax.experimental.pallas import tpu as pltpu
from jax.sharding import Mesh
from jax.sharding import PartitionSpec as P

F32 = jnp.float32
BF16 = jnp.bfloat16
I32 = jnp.int32
HIGH = lax.Precision.HIGHEST
NT = (((1,), (1,)), ((), ()))

DP = ("dp_0", "dp_1")
DP_EXPERT_TENSOR = ("dp_0", "dp_1", "expert", "tensor")
DP_EXPERT = ("dp_0", "dp_1", "expert")
EXPERT_TENSOR_DP = ("expert", "tensor", "dp_0", "dp_1")

NY, NC, NZ, NX = 8, 2, 12, 4
NE = 8
CAP = 9
TOK = 32
NQ = 4
LB = 4
QC = LB * 128
RP = 40
RX = 112
ROWS = NX * RX
ZORDER = (6, 7, 5, 8, 4, 9, 3, 10, 2, 11, 1)
PLUS, MINUS = 0, 1
RS_SLOT = {}
for _s in range(4):
    for _dir, _half, _n in ((PLUS, 0, 4), (MINUS, 1, 4), (PLUS, 1, 3), (MINUS, 0, 3)):
        if _s < _n:
            RS_SLOT[(_dir, _half, _s)] = len(RS_SLOT)
NRS = len(RS_SLOT)


def iota(shape, dim):
    return lax.broadcasted_iota(I32, shape, dim)


def onehot(mask):
    return jnp.where(mask, 1.0, 0.0).astype(BF16)


def dot(a, b, dims=(((1,), (0,)), ((), ())), precision=None):
    return lax.dot_general(a, b, dims, precision=precision, preferred_element_type=F32)


def kernel(
    ids_ref, rin_ref, rwt_ref, grad_ref, down_hbm, hid_hbm,
    wg_ref, hg_hbm, rg_ref, ig_ref,
    down, hid, hidp, hidt, image, hg, gcol, relay_r,
    chunk, zbuf, xsend, xbuf,
    logit_buf, pg_send, pg_buf, pgx_send, pgx_buf,
    gx_send, gx_buf, gz_send, gz_buf, lg_buf,
    rp_send, rc_buf, ry_send, ry_buf, rz_send, rz_buf, rx_send, rx_buf,
    wbuf, dbuf, rsbuf,
    load_sem, out_sem,
    zs_sem, zr_sem, xs_sem, xr_sem,
    small_s, small_r,
    d_s, d_r, rs_s, rs_r,
):
    y, c = lax.axis_index("dp_0"), lax.axis_index("dp_1")
    z, x = lax.axis_index("expert"), lax.axis_index("tensor")
    oc = 1 - c
    e_lo, e_hi = (z * NX) // 6, (z * NX + NX - 1) // 6
    middle = lax.rem(z, 3) == 1
    sel_hi = lax.rem(z, 3) * (2 - lax.rem(z, 3))
    zpeers = [lax.rem(z + k, NZ) for k in ZORDER]
    xpeers = [lax.rem(x + k, NX) for k in (2, 1, 3)]
    ypeers = [lax.rem(y + k, NY) for k in (4, 5, 3, 6, 2, 7, 1)]
    up, dn = lax.rem(y + 1, NY), lax.rem(y + NY - 1, NY)

    def load(src, dst, i):
        return pltpu.make_async_copy(src, dst, load_sem.at[i])

    load(hid_hbm, hid, 0).start()
    load(down_hbm, down, 1).start()

    def send(src, dst, s_sem, r_sem, **where):
        pltpu.make_async_remote_copy(
            src_ref=src, dst_ref=dst, send_sem=s_sem, recv_sem=r_sem,
            device_id=where, device_id_type=pl.DeviceIdType.MESH,
        ).start()

    def wait(ref, sem):
        pltpu.make_async_copy(ref, ref, sem).wait()

    barrier = pltpu.get_barrier_semaphore()

    def greet(**where):
        pl.semaphore_signal(barrier, inc=1, device_id=where, device_id_type=pl.DeviceIdType.MESH)

    for p in zpeers:
        greet(expert=p)
    for p in xpeers:
        greet(tensor=p)
        greet(tensor=p, dp_1=oc)
    for p in ypeers:
        greet(dp_0=p)
    greet(dp_1=oc)

    sub8, lane8 = iota((8, 128), 0), iota((8, 128), 1)
    ids = [ids_ref[0:1, :], ids_ref[1:2, :]]
    hit = [sub8 == ids[k] for k in range(2)]
    hits = (jnp.where(hit[0], 1.0, 0.0) + jnp.where(hit[1], 1.0, 0.0)).astype(BF16)
    r128, l128 = iota((128, 128), 0), iota((128, 128), 1)
    tri = onehot((r128 < l128) & (r128 // TOK == l128 // TOK))
    before = dot(hits, tri)
    pos = [jnp.sum(jnp.where(hit[k], before, 0.0), axis=0, keepdims=True).astype(I32) for k in range(2)]
    lane1 = iota((1, 128), 1)
    target = [ids[k] * RP + (lane1 // TOK) * CAP + pos[k] for k in range(2)]
    slot_at = [r128 == pos[k] for k in range(2)]
    part = dot(rwt_ref[:, pl.ds(pl.multiple_of(x * 512, 512), 512)], rin_ref[...], NT)
    logit_buf[x] = part
    pack_rows = iota((NE * RP, 128), 0)
    table = onehot((pack_rows == target[0]) | (pack_rows == target[1]))
    for q in range(NQ):
        stack = jnp.concatenate(
            [grad_ref[:, q * QC + b * 128 : q * QC + (b + 1) * 128] for b in range(LB)], axis=0
        )
        packed = dot(table, stack).astype(BF16)
        for e in range(NE):
            chunk[q, e] = packed[e * RP : (e + 1) * RP]

    pl.semaphore_wait(barrier, len(zpeers) + 2 * len(xpeers) + len(ypeers) + 1)

    for p in xpeers:
        send(logit_buf.at[x], logit_buf.at[x], small_s.at[0], small_r.at[0], tensor=p)

    def z_send(q):
        for p in zpeers:
            lo, hi = (p * NX) // 6, (p * NX + NX - 1) // 6
            send(chunk.at[q, lo], zbuf.at[0, q, z], zs_sem.at[0, q], zr_sem.at[0, q], expert=p)

            @pl.when(lax.rem(p, 3) == 1)
            def _():
                send(chunk.at[q, hi], zbuf.at[1, q, z], zs_sem.at[1, q], zr_sem.at[1, q], expert=p)

    z_send(0)
    for q in range(NQ):
        zbuf[0, q, z] = chunk[q, e_lo]
        zbuf[1, q, z] = chunk[q, e_hi]

    others = lambda ref, n: ref.at[0 : n - 1]
    wait(others(logit_buf, NX), small_r.at[0])
    logits = logit_buf[0] + logit_buf[1] + logit_buf[2] + logit_buf[3]
    picked = [jnp.sum(jnp.where(hit[k], logits, 0.0), axis=0, keepdims=True) for k in range(2)]
    own_lanes = lane1 // TOK == x

    def spread(row):
        row = jnp.broadcast_to(jnp.where(own_lanes, row, 0.0), (8, 128))
        row = row + pltpu.roll(row, TOK, 1)
        return row + pltpu.roll(row, 2 * TOK, 1)

    gate = [
        spread(jax.nn.sigmoid(picked[0] - picked[1])),
        spread(jax.nn.sigmoid(picked[1] - picked[0])),
    ]
    first = lane8 < TOK
    packed_gate = dot(
        jnp.where(hit[0] & first, gate[0], 0.0).astype(BF16), onehot(slot_at[0]), NT
    ) + dot(jnp.where(hit[1] & first, gate[1], 0.0).astype(BF16), onehot(slot_at[1]), NT)
    pg_send[...] = packed_gate
    pg_buf[z] = packed_gate
    for p in zpeers:
        send(pg_send, pg_buf.at[z], small_s.at[1], small_r.at[1], expert=p)
    z_send(1)
    z_send(2)
    z_send(3)

    rr, kk = iota((RX, NZ * RP), 0), iota((RX, NZ * RP), 1)
    for b in range(LB):
        relay_r[b] = onehot((kk == (rr // CAP) * RP + b * CAP + lax.rem(rr, CAP)) & (rr < NZ * CAP))

    def z_relay(q):
        wait(others(zbuf.at[0, q], NZ), zr_sem.at[0, q])

        @pl.when(middle)
        def _():
            wait(others(zbuf.at[1, q], NZ), zr_sem.at[1, q])

        for cls in range(2):
            rows = zbuf[0 if cls == 0 else sel_hi, q].reshape(NZ * RP, 128)
            for b in range(LB):
                xsend[cls, q, :, b * 128 : (b + 1) * 128] = dot(relay_r[b], rows).astype(BF16)
        for p in xpeers:
            send(xsend.at[p // 2, q], xbuf.at[q, x], xs_sem.at[q], xr_sem.at[q], tensor=p)
        xbuf[q, x] = xsend[x // 2, q]

    load(hid_hbm, hid, 0).wait()
    r1, m1 = iota((ROWS, NX * NZ * CAP), 0), iota((ROWS, NX * NZ * CAP), 1)
    in_col = lax.rem(r1, RX)
    perm = onehot(
        (m1 == ((in_col // CAP) * NX + r1 // RX) * CAP + lax.rem(in_col, CAP)) & (in_col < NZ * CAP)
    )
    hidp[...] = dot(perm, hid[...]).astype(BF16)
    hidt[...] = hidp[...].T

    z_relay(0)

    wait(others(pg_buf, NZ), small_r.at[1])
    sub3 = iota((NZ, 8, 128), 1)
    for cls, e in ((0, e_lo), (1, e_hi)):
        pgx_send[cls] = jnp.zeros((16, 128), F32)
        pgx_send[cls, 0:NZ] = jnp.sum(jnp.where(sub3 == e, pg_buf[...], 0.0), axis=1)
    for p in xpeers:
        send(pgx_send.at[p // 2], pgx_buf.at[x], small_s.at[2], small_r.at[2], tensor=p)
    pgx_buf[x] = pgx_send[x // 2]

    z_relay(1)

    rq, lq = iota((ROWS, 64), 0), iota((ROWS, 64), 1)
    qc = lax.rem(rq, RX)
    column_of = onehot((lq == (rq // RX) * 16 + qc // CAP) & (qc < NZ * CAP))
    rw, lw = iota((ROWS, 128), 0), iota((ROWS, 128), 1)
    own_slot = lw == lax.rem(lax.rem(rw, RX), CAP)

    def make_gates():
        wait(others(pgx_buf, NX), small_r.at[2])
        spread_gate = dot(column_of, pgx_buf[...].reshape(64, 128).astype(BF16))
        column = jnp.sum(jnp.where(own_slot, spread_gate, 0.0), axis=1, keepdims=True)
        gcol[...] = jnp.broadcast_to(column, (ROWS, 128))

    def x_wait(q):
        wait(others(xbuf.at[q], NX), xr_sem.at[q])

    def image_part(q):
        part = dot(xbuf[q].reshape(ROWS, QC), down[:, q * QC : (q + 1) * QC], NT)
        if q == 0:
            image[...] = part
        else:
            image[...] += part

    def weight_part(q):
        rows = xbuf[q].reshape(ROWS, QC).astype(F32)
        gated = (gcol[:, 0:1] * rows).astype(BF16)
        term = dot(hidt[...], gated).astype(BF16)
        for yy in range(NY):
            for cc in range(NC):
                at = (yy * NC + cc) * 80
                wbuf[q, cc, yy] = term[at : at + 80]
        send(wbuf.at[q, oc], dbuf.at[q], d_s.at[q], d_r.at[q], dp_1=oc)

    def cols(half):
        return pl.ds(half * (QC // 2), QC // 2)

    def y_send(q, src, d, half, s):
        slot = RS_SLOT[(d, half, s)]
        send(src, rsbuf.at[q, slot], rs_s.at[q], rs_r.at[q, slot], dp_0=up if d == PLUS else dn)

    def rs_first(q):
        wait(dbuf.at[q], d_r.at[q])
        dbuf[q] = (wbuf[q, c].astype(F32) + dbuf[q].astype(F32)).astype(BF16)
        for d, half, far in ((PLUS, 0, 4), (MINUS, 1, 4), (PLUS, 1, 3), (MINUS, 0, 5)):
            y_send(q, dbuf.at[q, lax.rem(y + far, NY), :, cols(half)], d, half, 0)

    def rs_step(q, s):
        for d, half, n, off in (
            (PLUS, 0, 4, 3 - s), (MINUS, 1, 4, 5 + s), (PLUS, 1, 3, 2 - s), (MINUS, 0, 3, 6 + s),
        ):
            if s >= n:
                continue
            slot = RS_SLOT[(d, half, s)]
            wait(rsbuf.at[q, slot], rs_r.at[q, slot])
            if s == n - 1:
                continue
            block = dbuf[q, lax.rem(y + off, NY), :, half * (QC // 2) : (half + 1) * (QC // 2)]
            rsbuf[q, slot] = (rsbuf[q, slot].astype(F32) + block.astype(F32)).astype(BF16)
            y_send(q, rsbuf.at[q, slot], d, half, s + 1)
        if s == 3:
            for half in range(2):
                lo = half * (QC // 2)
                a = rsbuf[q, RS_SLOT[(PLUS, half, 3 - half)]].astype(F32)
                b = rsbuf[q, RS_SLOT[(MINUS, half, 2 + half)]].astype(F32)
                mine = dbuf[q, y, :, lo : lo + QC // 2].astype(F32)
                wg_ref[:, q * QC + lo : q * QC + lo + QC // 2] = (mine + a + b).astype(BF16)

    make_gates()
    x_wait(0)
    weight_part(0)
    load(down_hbm, down, 1).wait()
    image_part(0)
    z_relay(2)
    rs_first(0)
    x_wait(1)
    weight_part(1)
    image_part(1)
    z_relay(3)
    rs_step(0, 0)
    rs_first(1)
    x_wait(2)
    image_part(2)
    weight_part(2)
    rs_step(0, 1)
    rs_step(1, 0)
    x_wait(3)
    image_part(3)

    slot_sum = jnp.sum(hidp[...].astype(F32) * image[...], axis=1, keepdims=True)
    rt, lt = iota((64, ROWS), 0), iota((64, ROWS), 1)
    tc = lax.rem(lt, RX)
    back = jnp.where((rt == (lt // RX) * 16 + tc // CAP) & (tc < NZ * CAP), 1.0, 0.0)
    slots = dot(back, jnp.where(own_slot, slot_sum, 0.0), precision=HIGH)
    for p in range(NX):
        gx_send[p] = slots[p * 16 : (p + 1) * 16]
    gx_buf[x] = gx_send[x]
    for p in xpeers:
        send(gx_send.at[p], gx_buf.at[x], small_s.at[3], small_r.at[3], tensor=p)

    weight_part(3)
    rs_first(2)

    wait(others(gx_buf, NX), small_r.at[3])
    sum_lo, sum_hi = gx_buf[0] + gx_buf[1], gx_buf[2] + gx_buf[3]
    for p in range(NZ):
        gz_send[p] = jnp.where(sub8 == e_lo, sum_lo[p : p + 1], 0.0) + jnp.where(
            sub8 == e_hi, sum_hi[p : p + 1], 0.0
        )
    gz_buf[z] = gz_send[z]
    for p in zpeers:
        send(gz_send.at[p], gz_buf.at[z], small_s.at[4], small_r.at[4], expert=p)

    rs_step(0, 2)
    rs_step(1, 1)
    rs_first(3)

    scaled = (gcol[:, 0:1] * image[...]).astype(BF16)
    m2, r2 = iota((NX * NZ * CAP, ROWS), 0), iota((NX * NZ * CAP, ROWS), 1)
    unperm = onehot(r2 == lax.rem(m2 // CAP, NX) * RX + (m2 // (CAP * NX)) * CAP + lax.rem(m2, CAP))
    hg[...] = dot(unperm, scaled).astype(BF16)
    out_copy = pltpu.make_async_copy(hg, hg_hbm, out_sem)
    out_copy.start()

    rs_step(2, 0)

    wait(others(gz_buf, NZ), small_r.at[4])
    sums = gz_buf[0]
    for p in range(1, NZ):
        sums = sums + gz_buf[p]
    gate_grad = []
    for k in range(2):
        at_slot = dot(sums, jnp.where(slot_at[k], 1.0, 0.0), precision=HIGH)
        gate_grad.append(jnp.sum(jnp.where(hit[k], at_slot, 0.0), axis=0, keepdims=True))
    mixed = gate[0] * gate_grad[0] + gate[1] * gate_grad[1]
    logit_grad = jnp.where(hit[0], gate[0] * (gate_grad[0] - mixed), 0.0) + jnp.where(
        hit[1], gate[1] * (gate_grad[1] - mixed), 0.0
    )
    lg_buf[x] = jnp.where(lane8 // TOK == x, logit_grad, 0.0)
    for p in xpeers:
        send(lg_buf.at[x], lg_buf.at[x], small_s.at[5], small_r.at[5], tensor=p)
    tall = jnp.where(r128 // 8 == 0, jnp.concatenate([logit_grad] * 16, axis=0), 0.0).T
    ig_ref[...] = dot(tall[0:TOK, 0:8], rwt_ref[...].astype(F32), precision=HIGH).astype(BF16)

    rs_step(0, 3)
    rs_step(1, 2)

    wait(others(lg_buf, NX), small_r.at[5])
    group_grad = lg_buf[0] + lg_buf[1] + lg_buf[2] + lg_buf[3]
    router = dot(group_grad, rin_ref[...].astype(F32), precision=HIGH)
    rp_send[0] = router[:, 0:256]
    rp_send[1] = router[:, 256:512]
    send(rp_send.at[oc], rc_buf, small_s.at[6], small_r.at[6], dp_1=oc)

    rs_step(2, 1)
    rs_step(3, 0)

    wait(rc_buf, small_r.at[6])
    pair = rp_send[c] + rc_buf[...]
    ry_send[...] = pair
    ry_buf[y] = pair
    for p in ypeers:
        send(ry_send, ry_buf.at[y], small_s.at[7], small_r.at[7], dp_0=p)
    rs_step(1, 3)
    rs_step(2, 2)
    wait(others(ry_buf, NY), small_r.at[7])
    total = ry_buf[0]
    for p in range(1, NY):
        total = total + ry_buf[p]
    rz_send[...] = total
    rz_buf[z] = total
    for p in zpeers:
        send(rz_send, rz_buf.at[z], small_s.at[8], small_r.at[8], expert=p)
    rs_step(3, 1)
    rs_step(2, 3)
    wait(others(rz_buf, NZ), small_r.at[8])
    total = rz_buf[0]
    for p in range(1, NZ):
        total = total + rz_buf[p]
    rx_send[...] = total
    here = x * NC + c
    rx_buf[here] = total
    for p in xpeers:
        for cc in (c, oc):
            send(rx_send, rx_buf.at[here], small_s.at[9], small_r.at[9], tensor=p, dp_1=cc)
    send(rx_send, rx_buf.at[here], small_s.at[9], small_r.at[9], dp_1=oc)
    rs_step(3, 2)
    rs_step(3, 3)
    wait(others(rx_buf, NX * NC), small_r.at[9])
    rg_ref[...] = rx_buf[...]

    for q in range(NQ):
        wait(others(zbuf.at[0, q], NZ), zs_sem.at[0, q])

        @pl.when(middle)
        def _():
            wait(zbuf.at[1, q, 0:3], zs_sem.at[1, q])

        @pl.when(jnp.logical_not(middle))
        def _():
            wait(zbuf.at[1, q, 0:4], zs_sem.at[1, q])

        wait(others(xbuf.at[q], NX), xs_sem.at[q])
        wait(dbuf.at[q], d_s.at[q])
        wait(rsbuf.at[q], rs_s.at[q])
    wait(others(logit_buf, NX), small_s.at[0])
    wait(others(pg_buf, NZ), small_s.at[1])
    wait(others(pgx_buf, NX), small_s.at[2])
    wait(others(gx_buf, NX), small_s.at[3])
    wait(others(gz_buf, NZ), small_s.at[4])
    wait(others(lg_buf, NX), small_s.at[5])
    wait(rc_buf, small_s.at[6])
    wait(others(ry_buf, NY), small_s.at[7])
    wait(others(rz_buf, NZ), small_s.at[8])
    wait(others(rx_buf, NX * NC), small_s.at[9])
    out_copy.wait()


def per_device(router_input, router_weight, expert_ids, down_weight, hidden, grad_output):
    ids = jnp.pad(jnp.tile(expert_ids.T, (1, 128 // TOK)), ((0, 6), (0, 0)))
    rwt = router_weight.T
    slots, units = hidden.shape[1], hidden.shape[2]
    width = grad_output.shape[1]
    vmem = pl.BlockSpec(memory_space=pltpu.VMEM)
    hbm = pl.BlockSpec(memory_space=pl.ANY)
    V = pltpu.VMEM
    dma = pltpu.SemaphoreType.DMA
    weight_grad, hidden_grad, router, input_grad = pl.pallas_call(
        kernel,
        out_shape=(
            jax.ShapeDtypeStruct((units // (NY * NC), width), BF16),
            jax.ShapeDtypeStruct((slots, units), BF16),
            jax.ShapeDtypeStruct((NX * NC, 8, 256), F32),
            jax.ShapeDtypeStruct((TOK, width), BF16),
        ),
        in_specs=[vmem, vmem, vmem, vmem, hbm, hbm],
        out_specs=(vmem, hbm, vmem, vmem),
        scratch_shapes=[
            V((units, width), BF16),
            V((slots, units), BF16),
            V((ROWS, units), BF16),
            V((units, ROWS), BF16),
            V((ROWS, units), F32),
            V((slots, units), BF16),
            V((ROWS, 128), F32),
            V((LB, RX, NZ * RP), BF16),
            V((NQ, NE, RP, 128), BF16),
            V((2, NQ, NZ, RP, 128), BF16),
            V((2, NQ, RX, QC), BF16),
            V((NQ, NX, RX, QC), BF16),
            V((NX, 8, 128), F32),
            V((8, 128), F32),
            V((NZ, 8, 128), F32),
            V((2, 16, 128), F32),
            V((NX, 16, 128), F32),
            V((NX, 16, 128), F32),
            V((NX, 16, 128), F32),
            V((NZ, 8, 128), F32),
            V((NZ, 8, 128), F32),
            V((NX, 8, 128), F32),
            V((2, 8, 256), F32),
            V((8, 256), F32),
            V((8, 256), F32),
            V((NY, 8, 256), F32),
            V((8, 256), F32),
            V((NZ, 8, 256), F32),
            V((8, 256), F32),
            V((NX * NC, 8, 256), F32),
            V((NQ, NC, NY, 80, QC), BF16),
            V((NQ, NY, 80, QC), BF16),
            V((NQ, NRS, 80, QC // 2), BF16),
            dma((2,)), dma,
            dma((2, NQ)), dma((2, NQ)), dma((NQ,)), dma((NQ,)),
            dma((10,)), dma((10,)),
            dma((NQ,)), dma((NQ,)), dma((NQ,)), dma((NQ, NRS)),
        ],
        compiler_params=pltpu.CompilerParams(
            collective_id=0, has_side_effects=True, vmem_limit_bytes=60 * 1024 * 1024
        ),
    )(ids, router_input, rwt, grad_output, down_weight, hidden[0])
    router_grad = jnp.transpose(router, (0, 2, 1)).reshape(width, 8)
    return weight_grad, hidden_grad[None], router_grad, input_grad


def solution(mesh):
    finer = Mesh(
        mesh.devices.reshape(NY, NC, mesh.shape["expert"], mesh.shape["tensor"]),
        ("dp_0", "dp_1", "expert", "tensor"),
    )
    placed = (
        P(DP_EXPERT, "tensor"),
        P(),
        P(DP_EXPERT_TENSOR, None),
        P(("expert", "tensor"), None),
        P(DP, None, ("expert", "tensor")),
        P(DP_EXPERT_TENSOR, None),
    )
    return jax.shard_map(
        per_device,
        mesh=finer,
        in_specs=placed,
        out_specs=(
            P(EXPERT_TENSOR_DP, None),
            P(DP, None, ("expert", "tensor")),
            P(),
            P(DP_EXPERT_TENSOR, None),
        ),
        check_vma=False,
    )
```

time: 515 us -> 98.1 us (0.19)
  waiting for transfers between devices: 409 us -> 0 us
  Pallas kernels: 0 us -> 90.5 us
  starting transfers between devices: 26 us -> 0 us
  blocking collectives: 23.7 us -> 0 us
  matrix products: 15.1 us -> 0 us
  between operations: 15.4 us -> 0.64 us
  local copies, waits for them, and re-layouts: 20 us -> 6.72 us
    psum x4 -> x0, waiting for transfers between devices: 271 us -> none  [by_axis(): return functools.reduce(lax.psum, axes, array)]
    all_to_all x3 -> x0, waiting for transfers between devices: 114 us -> none  [the longest x1 101 us: per_device(): lax.all_to_all(send_grad, ('expert', 'tensor'), split_axis=0, concat_axis...]
    pallas_call x0 -> x1, Pallas kernels: none -> 90.5 us  [per_device(): pl.pallas_call(kernel, out_shape=(jax.ShapeDtypeStruct((units // (NY * NC...]
    all_to_all x3 -> x0, starting transfers between devices: 25.8 us -> none  [the longest x1 16.2 us: per_device(): lax.all_to_all(send_gate, ('expert', 'tensor'), split_axis=0, concat_axis...]
    unnamed x6 -> x0, waiting for transfers between devices: 24.1 us -> none
    all_to_all x1 -> x0, blocking collectives: 23.7 us -> none  [per_device(): lax.all_to_all(gate_partial, ('expert', 'tensor'), split_axis=0, concat_a...]
    dot_general x8 -> x0, matrix products: 15.1 us -> none  [the longest x1 6.84 us: per_device(): lax.dot_general(recv_grad, down_weight, (((1,), (1,)), ((), ())), preferr...]
    unnamed x11 -> x8, local copies, waits for them, and re-layouts: 10.9 us -> 5.35 us
  transfers between devices with their start and end apart: 8 -> 0, of which waited for: 8 -> 0; matrix products, arithmetic and copies ran while one was open for 4% -> 0% of each run, Pallas kernels for 0% -> 0%
where the time goes in v1:
time: 98.1 us; the launch traced here: 97.8 us
  Pallas kernels  90.5 us (92%)
  local copies, waits for them, and re-layouts  6.72 us (7%)
    pallas_call x1, Pallas kernels, per_device(): pl.pallas_call(kernel, out_shape=(jax.ShapeDtypeStruct((units // (NY * NC...  90.5 us
    unnamed x8, local copies, waits for them, and re-layouts  5.35 us

profile of v1, /device:TPU:1, one launch (start us, length us, event | category | flops | bytes accessed | tf_op | source)
XLA Modules:
  0.0 97.8 jit_solution(18183783771679049555)
XLA Ops:
  0.6 0.7 tile.4
  1.3 0.1 tile.10
  1.4 0.6 pad.4.ids_ref
  2.0 90.5 %shard_map.93 = (bf16[80,2048]{1,0:T(8,128)(2,1)}, bf16[432,1280]{1,0:T(8,128)(2,1)}, f32[8,8,256]{2,1,0:T(8,128)}, bf16[32,2048]{1,0:T(8,128)(2,1)}) custom-call(s32[8,128]{1,0:T(8,128)} %pad.4.ids_ref, bf16[128,512]{1,0:T(8,128)(2,1)} %rin_ref.1, bf16[8,2048]{1,0:T(8,128)(2,1)} %bitcast.10, bf16[32,2048]{1,0:T(8,128)(2,1)} %grad_ref.1, ...), custom_call_target="tpu_custom_call" | custom-call | tf_op jit(solution)/shard_map/pallas_call | solution.py:443
  92.5 1.7 %copy.14 = bf16[80,2048]{1,0:T(8,128)(2,1)} copy(bf16[80,2048]{1,0:T(8,128)(2,1)} %get-tuple-element.16) | data formatting | bytes 655360
  94.2 0.0 copy-start.1
  94.2 0.0 copy-start
  94.2 2.3 %copy.15 = bf16[1,432,1280]{2,1,0:T(8,128)(2,1)} copy(bf16[1,432,1280]{2,1,0:T(8,128)(2,1)} %bitcast.8) | data formatting | bytes 2211840
  96.5 0.0 copy-done.1
  96.6 0.6 copy.16
  97.2 0.0 copy-done
  97.2 0.7 copy.17
Async XLA Ops:
  94.2 2.4 %copy-start.1 = (f32[8,8,256]{2,1,0:T(8,128)S(1)}, f32[8,8,256]{2,1,0:T(8,128)}, u32[]{:S(2)}) copy-start(f32[8,8,256]{2,1,0:T(8,128)} %get-tuple-element.10) | copy-start | bytes 196612
  94.2 3.0 %copy-start = (bf16[32,2048]{1,0:T(8,128)(2,1)S(1)}, bf16[32,2048]{1,0:T(8,128)(2,1)}, u32[]{:S(2)}) copy-start(bf16[32,2048]{1,0:T(8,128)(2,1)} %get-tuple-element.19) | copy-start | bytes 393220

commit v2 on v1

--- a/solution.py
+++ b/solution.py
@@ -53,14 +53,14 @@
 
 def kernel(
     ids_ref, rin_ref, rwt_ref, grad_ref, down_hbm, hid_hbm,
-    wg_ref, hg_hbm, rg_ref, ig_ref,
-    down, hid, hidp, hidt, image, hg, gcol, relay_r,
+    wg_ref, hg, rg_ref, ig_ref,
+    down, hid, hidp, hidt, image, gcol, relay_r, ids_v, tall,
     chunk, zbuf, xsend, xbuf,
     logit_buf, pg_send, pg_buf, pgx_send, pgx_buf,
-    gx_send, gx_buf, gz_send, gz_buf, lg_buf,
-    rp_send, rc_buf, ry_send, ry_buf, rz_send, rz_buf, rx_send, rx_buf,
+    gx_buf, gz_buf,
+    rp_send, rc_buf, ry_buf, rz_buf, rx_buf,
     wbuf, dbuf, rsbuf,
-    load_sem, out_sem,
+    load_sem,
     zs_sem, zr_sem, xs_sem, xr_sem,
     small_s, small_r,
     d_s, d_r, rs_s, rs_r,
@@ -105,8 +105,10 @@
         greet(dp_0=p)
     greet(dp_1=oc)
 
-    sub8, lane8 = iota((8, 128), 0), iota((8, 128), 1)
-    ids = [ids_ref[0:1, :], ids_ref[1:2, :]]
+    for b in range(128 // TOK):
+        ids_v[0:2, b * TOK : (b + 1) * TOK] = ids_ref[...]
+    sub8 = iota((8, 128), 0)
+    ids = [ids_v[0:1, :], ids_v[1:2, :]]
     hit = [sub8 == ids[k] for k in range(2)]
     hits = (jnp.where(hit[0], 1.0, 0.0) + jnp.where(hit[1], 1.0, 0.0)).astype(BF16)
     r128, l128 = iota((128, 128), 0), iota((128, 128), 1)
@@ -114,13 +116,12 @@
     before = dot(hits, tri)
     pos = [jnp.sum(jnp.where(hit[k], before, 0.0), axis=0, keepdims=True).astype(I32) for k in range(2)]
     lane1 = iota((1, 128), 1)
+    own_lanes = lane1 // TOK == x
     target = [ids[k] * RP + (lane1 // TOK) * CAP + pos[k] for k in range(2)]
-    slot_at = [r128 == pos[k] for k in range(2)]
-    part = dot(rwt_ref[:, pl.ds(pl.multiple_of(x * 512, 512), 512)], rin_ref[...], NT)
-    logit_buf[x] = part
     pack_rows = iota((NE * RP, 128), 0)
     table = onehot((pack_rows == target[0]) | (pack_rows == target[1]))
-    for q in range(NQ):
+
+    def pack(q):
         stack = jnp.concatenate(
             [grad_ref[:, q * QC + b * 128 : q * QC + (b + 1) * 128] for b in range(LB)], axis=0
         )
@@ -128,6 +129,13 @@
         for e in range(NE):
             chunk[q, e] = packed[e * RP : (e + 1) * RP]
 
+    pack(0)
+    logit_buf[x, 0:8] = dot(rwt_ref[:, pl.ds(pl.multiple_of(x * 512, 512), 512)], rin_ref[...], NT)
+    info = jnp.zeros((8, 128), F32)
+    for row, value in enumerate(ids + pos):
+        info = jnp.where(sub8 == row, jnp.where(own_lanes, value.astype(F32), 0.0), info)
+    logit_buf[x, 8:16] = info
+
     pl.semaphore_wait(barrier, len(zpeers) + 2 * len(xpeers) + len(ypeers) + 1)
 
     for p in xpeers:
@@ -143,29 +151,24 @@
                 send(chunk.at[q, hi], zbuf.at[1, q, z], zs_sem.at[1, q], zr_sem.at[1, q], expert=p)
 
     z_send(0)
+    for q in range(1, NQ):
+        pack(q)
     for q in range(NQ):
         zbuf[0, q, z] = chunk[q, e_lo]
         zbuf[1, q, z] = chunk[q, e_hi]
 
     others = lambda ref, n: ref.at[0 : n - 1]
     wait(others(logit_buf, NX), small_r.at[0])
-    logits = logit_buf[0] + logit_buf[1] + logit_buf[2] + logit_buf[3]
+    shared = logit_buf[0] + logit_buf[1] + logit_buf[2] + logit_buf[3]
+    logits = shared[0:8]
+    ids = [shared[8 + k : 9 + k].astype(I32) for k in range(2)]
+    pos = [shared[10 + k : 11 + k].astype(I32) for k in range(2)]
+    hit = [sub8 == ids[k] for k in range(2)]
     picked = [jnp.sum(jnp.where(hit[k], logits, 0.0), axis=0, keepdims=True) for k in range(2)]
-    own_lanes = lane1 // TOK == x
-
-    def spread(row):
-        row = jnp.broadcast_to(jnp.where(own_lanes, row, 0.0), (8, 128))
-        row = row + pltpu.roll(row, TOK, 1)
-        return row + pltpu.roll(row, 2 * TOK, 1)
-
-    gate = [
-        spread(jax.nn.sigmoid(picked[0] - picked[1])),
-        spread(jax.nn.sigmoid(picked[1] - picked[0])),
-    ]
-    first = lane8 < TOK
+    gate = [jax.nn.sigmoid(picked[0] - picked[1]), jax.nn.sigmoid(picked[1] - picked[0])]
     packed_gate = dot(
-        jnp.where(hit[0] & first, gate[0], 0.0).astype(BF16), onehot(slot_at[0]), NT
-    ) + dot(jnp.where(hit[1] & first, gate[1], 0.0).astype(BF16), onehot(slot_at[1]), NT)
+        jnp.where(hit[0] & own_lanes, gate[0], 0.0).astype(BF16), onehot(r128 == pos[0]), NT
+    ) + dot(jnp.where(hit[1] & own_lanes, gate[1], 0.0).astype(BF16), onehot(r128 == pos[1]), NT)
     pg_send[...] = packed_gate
     pg_buf[z] = packed_gate
     for p in zpeers:
@@ -303,28 +306,20 @@
     image_part(3)
 
     slot_sum = jnp.sum(hidp[...].astype(F32) * image[...], axis=1, keepdims=True)
-    rt, lt = iota((64, ROWS), 0), iota((64, ROWS), 1)
-    tc = lax.rem(lt, RX)
-    back = jnp.where((rt == (lt // RX) * 16 + tc // CAP) & (tc < NZ * CAP), 1.0, 0.0)
-    slots = dot(back, jnp.where(own_slot, slot_sum, 0.0), precision=HIGH)
-    for p in range(NX):
-        gx_send[p] = slots[p * 16 : (p + 1) * 16]
-    gx_buf[x] = gx_send[x]
+    rt, lt = iota((8, ROWS), 0), iota((8, ROWS), 1)
+    back = jnp.where(rt == (x // 2) * sel_hi * NX + lt // RX, 1.0, 0.0)
+    own_row = (lw == lax.rem(rw, RX)) & (lw < NZ * CAP)
+    gx_buf[x] = dot(back, jnp.where(own_row, slot_sum, 0.0), precision=HIGH)
     for p in xpeers:
-        send(gx_send.at[p], gx_buf.at[x], small_s.at[3], small_r.at[3], tensor=p)
+        send(gx_buf.at[x], gx_buf.at[x], small_s.at[3], small_r.at[3], tensor=p)
 
     weight_part(3)
     rs_first(2)
 
     wait(others(gx_buf, NX), small_r.at[3])
-    sum_lo, sum_hi = gx_buf[0] + gx_buf[1], gx_buf[2] + gx_buf[3]
-    for p in range(NZ):
-        gz_send[p] = jnp.where(sub8 == e_lo, sum_lo[p : p + 1], 0.0) + jnp.where(
-            sub8 == e_hi, sum_hi[p : p + 1], 0.0
-        )
-    gz_buf[z] = gz_send[z]
+    gz_buf[z] = gx_buf[0] + gx_buf[1] + gx_buf[2] + gx_buf[3]
     for p in zpeers:
-        send(gz_send.at[p], gz_buf.at[z], small_s.at[4], small_r.at[4], expert=p)
+        send(gz_buf.at[z], gz_buf.at[z], small_s.at[4], small_r.at[4], expert=p)
 
     rs_step(0, 2)
     rs_step(1, 1)
@@ -334,75 +329,71 @@
     m2, r2 = iota((NX * NZ * CAP, ROWS), 0), iota((NX * NZ * CAP, ROWS), 1)
     unperm = onehot(r2 == lax.rem(m2 // CAP, NX) * RX + (m2 // (CAP * NX)) * CAP + lax.rem(m2, CAP))
     hg[...] = dot(unperm, scaled).astype(BF16)
-    out_copy = pltpu.make_async_copy(hg, hg_hbm, out_sem)
-    out_copy.start()
 
     rs_step(2, 0)
 
     wait(others(gz_buf, NZ), small_r.at[4])
-    sums = gz_buf[0]
-    for p in range(1, NZ):
-        sums = sums + gz_buf[p]
+    sums = []
+    for p in range(0, NZ, 3):
+        sums.append(gz_buf[p] + gz_buf[p + 1])
+        sums.append(gz_buf[p + 2] + pltpu.roll(gz_buf[p + 1], 4, 0))
+    sums = jnp.concatenate(sums, axis=0)
+    r64 = iota((64, 128), 0)
     gate_grad = []
     for k in range(2):
-        at_slot = dot(sums, jnp.where(slot_at[k], 1.0, 0.0), precision=HIGH)
-        gate_grad.append(jnp.sum(jnp.where(hit[k], at_slot, 0.0), axis=0, keepdims=True))
+        at_slot = dot(sums, jnp.where(r128 == z * CAP + pos[k], 1.0, 0.0), precision=HIGH)
+        mine = r64 == ids[k] * 8 + lane1 // TOK
+        gate_grad.append(jnp.sum(jnp.where(mine, at_slot, 0.0), axis=0, keepdims=True))
     mixed = gate[0] * gate_grad[0] + gate[1] * gate_grad[1]
     logit_grad = jnp.where(hit[0], gate[0] * (gate_grad[0] - mixed), 0.0) + jnp.where(
         hit[1], gate[1] * (gate_grad[1] - mixed), 0.0
     )
-    lg_buf[x] = jnp.where(lane8 // TOK == x, logit_grad, 0.0)
-    for p in xpeers:
-        send(lg_buf.at[x], lg_buf.at[x], small_s.at[5], small_r.at[5], tensor=p)
-    tall = jnp.where(r128 // 8 == 0, jnp.concatenate([logit_grad] * 16, axis=0), 0.0).T
-    ig_ref[...] = dot(tall[0:TOK, 0:8], rwt_ref[...].astype(F32), precision=HIGH).astype(BF16)
+    router = dot(logit_grad, rin_ref[...].astype(F32), precision=HIGH)
+    rp_send[0] = router[:, 0:256]
+    rp_send[1] = router[:, 256:512]
+    send(rp_send.at[oc], rc_buf, small_s.at[5], small_r.at[5], dp_1=oc)
 
     rs_step(0, 3)
     rs_step(1, 2)
 
-    wait(others(lg_buf, NX), small_r.at[5])
-    group_grad = lg_buf[0] + lg_buf[1] + lg_buf[2] + lg_buf[3]
-    router = dot(group_grad, rin_ref[...].astype(F32), precision=HIGH)
-    rp_send[0] = router[:, 0:256]
-    rp_send[1] = router[:, 256:512]
-    send(rp_send.at[oc], rc_buf, small_s.at[6], small_r.at[6], dp_1=oc)
+    wait(rc_buf, small_r.at[5])
+    pair = rp_send[c] + rc_buf[...]
+    rz_buf[z] = pair
+    for p in zpeers:
+        send(rz_buf.at[z], rz_buf.at[z], small_s.at[6], small_r.at[6], expert=p)
 
     rs_step(2, 1)
     rs_step(3, 0)
-
-    wait(rc_buf, small_r.at[6])
-    pair = rp_send[c] + rc_buf[...]
-    ry_send[...] = pair
-    ry_buf[y] = pair
-    for p in ypeers:
-        send(ry_send, ry_buf.at[y], small_s.at[7], small_r.at[7], dp_0=p)
+    tall[...] = jnp.concatenate([logit_grad] * 16, axis=0).T
+    own_grad = tall[pl.ds(pl.multiple_of(x * TOK, TOK), TOK), 0:8]
+    ig_ref[...] = dot(own_grad, rwt_ref[...].astype(F32), precision=HIGH).astype(BF16)
     rs_step(1, 3)
     rs_step(2, 2)
+
+    wait(others(rz_buf, NZ), small_r.at[6])
+    total = rz_buf[0]
+    for p in range(1, NZ):
+        total = total + rz_buf[p]
+    ry_buf[y] = total
+    for p in ypeers:
+        send(ry_buf.at[y], ry_buf.at[y], small_s.at[7], small_r.at[7], dp_0=p)
+    rs_step(3, 1)
+    rs_step(2, 3)
     wait(others(ry_buf, NY), small_r.at[7])
     total = ry_buf[0]
     for p in range(1, NY):
         total = total + ry_buf[p]
-    rz_send[...] = total
-    rz_buf[z] = total
-    for p in zpeers:
-        send(rz_send, rz_buf.at[z], small_s.at[8], small_r.at[8], expert=p)
-    rs_step(3, 1)
-    rs_step(2, 3)
-    wait(others(rz_buf, NZ), small_r.at[8])
-    total = rz_buf[0]
-    for p in range(1, NZ):
-        total = total + rz_buf[p]
-    rx_send[...] = total
     here = x * NC + c
     rx_buf[here] = total
     for p in xpeers:
         for cc in (c, oc):
-            send(rx_send, rx_buf.at[here], small_s.at[9], small_r.at[9], tensor=p, dp_1=cc)
-    send(rx_send, rx_buf.at[here], small_s.at[9], small_r.at[9], dp_1=oc)
+            send(rx_buf.at[here], rx_buf.at[here], small_s.at[8], small_r.at[8], tensor=p, dp_1=cc)
+    send(rx_buf.at[here], rx_buf.at[here], small_s.at[8], small_r.at[8], dp_1=oc)
     rs_step(3, 2)
     rs_step(3, 3)
-    wait(others(rx_buf, NX * NC), small_r.at[9])
-    rg_ref[...] = rx_buf[...]
+    wait(others(rx_buf, NX * NC), small_r.at[8])
+    for i in range(NX * NC):
+        rg_ref[:, i * 256 : (i + 1) * 256] = rx_buf[i]
 
     for q in range(NQ):
         wait(others(zbuf.at[0, q], NZ), zs_sem.at[0, q])
@@ -418,21 +409,29 @@
         wait(others(xbuf.at[q], NX), xs_sem.at[q])
         wait(dbuf.at[q], d_s.at[q])
         wait(rsbuf.at[q], rs_s.at[q])
-    wait(others(logit_buf, NX), small_s.at[0])
-    wait(others(pg_buf, NZ), small_s.at[1])
-    wait(others(pgx_buf, NX), small_s.at[2])
-    wait(others(gx_buf, NX), small_s.at[3])
-    wait(others(gz_buf, NZ), small_s.at[4])
-    wait(others(lg_buf, NX), small_s.at[5])
-    wait(rc_buf, small_s.at[6])
+    for i, (buf, n) in enumerate(
+        ((logit_buf, NX), (pg_buf, NZ), (pgx_buf, NX), (gx_buf, NX), (gz_buf, NZ))
+    ):
+        wait(others(buf, n), small_s.at[i])
+    wait(rc_buf, small_s.at[5])
+    wait(others(rz_buf, NZ), small_s.at[6])
     wait(others(ry_buf, NY), small_s.at[7])
-    wait(others(rz_buf, NZ), small_s.at[8])
-    wait(others(rx_buf, NX * NC), small_s.at[9])
-    out_copy.wait()
+    wait(others(rx_buf, NX * NC), small_s.at[8])
+
+
+def write_out(wg, hg, rg, ig, wg_out, hg_out, rg_out, ig_out, sem):
+    copies = [
+        pltpu.make_async_copy(src, dst, sem.at[i])
+        for i, (src, dst) in enumerate(((hg, hg_out), (wg, wg_out), (ig, ig_out), (rg, rg_out)))
+    ]
+    for copy in copies:
+        copy.start()
+    for copy in copies:
+        copy.wait()
 
 
 def per_device(router_input, router_weight, expert_ids, down_weight, hidden, grad_output):
-    ids = jnp.pad(jnp.tile(expert_ids.T, (1, 128 // TOK)), ((0, 6), (0, 0)))
+    ids = expert_ids.T
     rwt = router_weight.T
     slots, units = hidden.shape[1], hidden.shape[2]
     width = grad_output.shape[1]
@@ -440,61 +439,64 @@
     hbm = pl.BlockSpec(memory_space=pl.ANY)
     V = pltpu.VMEM
     dma = pltpu.SemaphoreType.DMA
-    weight_grad, hidden_grad, router, input_grad = pl.pallas_call(
+    results = (
+        ((units // (NY * NC), width), BF16),
+        ((slots, units), BF16),
+        ((8, width), F32),
+        ((TOK, width), BF16),
+    )
+    inner = pl.pallas_call(
         kernel,
-        out_shape=(
-            jax.ShapeDtypeStruct((units // (NY * NC), width), BF16),
-            jax.ShapeDtypeStruct((slots, units), BF16),
-            jax.ShapeDtypeStruct((NX * NC, 8, 256), F32),
-            jax.ShapeDtypeStruct((TOK, width), BF16),
-        ),
+        out_shape=tuple(V(shape, kind) for shape, kind in results),
         in_specs=[vmem, vmem, vmem, vmem, hbm, hbm],
-        out_specs=(vmem, hbm, vmem, vmem),
+        out_specs=(vmem, vmem, vmem, vmem),
         scratch_shapes=[
             V((units, width), BF16),
             V((slots, units), BF16),
             V((ROWS, units), BF16),
             V((units, ROWS), BF16),
             V((ROWS, units), F32),
-            V((slots, units), BF16),
             V((ROWS, 128), F32),
             V((LB, RX, NZ * RP), BF16),
+            V((8, 128), I32),
+            V((128, 128), F32),
             V((NQ, NE, RP, 128), BF16),
             V((2, NQ, NZ, RP, 128), BF16),
             V((2, NQ, RX, QC), BF16),
             V((NQ, NX, RX, QC), BF16),
-            V((NX, 8, 128), F32),
+            V((NX, 16, 128), F32),
             V((8, 128), F32),
             V((NZ, 8, 128), F32),
             V((2, 16, 128), F32),
             V((NX, 16, 128), F32),
-            V((NX, 16, 128), F32),
-            V((NX, 16, 128), F32),
+            V((NX, 8, 128), F32),
             V((NZ, 8, 128), F32),
-            V((NZ, 8, 128), F32),
-            V((NX, 8, 128), F32),
             V((2, 8, 256), F32),
             V((8, 256), F32),
-            V((8, 256), F32),
             V((NY, 8, 256), F32),
-            V((8, 256), F32),
             V((NZ, 8, 256), F32),
-            V((8, 256), F32),
             V((NX * NC, 8, 256), F32),
             V((NQ, NC, NY, 80, QC), BF16),
             V((NQ, NY, 80, QC), BF16),
             V((NQ, NRS, 80, QC // 2), BF16),
-            dma((2,)), dma,
+            dma((2,)),
             dma((2, NQ)), dma((2, NQ)), dma((NQ,)), dma((NQ,)),
-            dma((10,)), dma((10,)),
+            dma((9,)), dma((9,)),
             dma((NQ,)), dma((NQ,)), dma((NQ,)), dma((NQ, NRS)),
         ],
         compiler_params=pltpu.CompilerParams(
             collective_id=0, has_side_effects=True, vmem_limit_bytes=60 * 1024 * 1024
         ),
     )(ids, router_input, rwt, grad_output, down_weight, hidden[0])
-    router_grad = jnp.transpose(router, (0, 2, 1)).reshape(width, 8)
-    return weight_grad, hidden_grad[None], router_grad, input_grad
+    weight_grad, hidden_grad, router, input_grad = pl.pallas_call(
+        write_out,
+        out_shape=tuple(jax.ShapeDtypeStruct(shape, kind) for shape, kind in results),
+        in_specs=[vmem] * 4,
+        out_specs=(hbm,) * 4,
+        scratch_shapes=[dma((4,))],
+        compiler_params=pltpu.CompilerParams(vmem_limit_bytes=1024 * 1024),
+    )(*inner)
+    return weight_grad, hidden_grad[None], router.T, input_grad
 
 
 def solution(mesh):

time: 98.1 us -> 86.2 us (0.88)
  local copies, waits for them, and re-layouts: 6.72 us -> 0 us
  Pallas kernels: 90.5 us -> 85.4 us
    unnamed x8 -> x0, local copies, waits for them, and re-layouts: 5.35 us -> none
    pallas_call x1 -> x2, Pallas kernels: 90.5 us -> 85.4 us  [the longest x1 84.2 us: per_device(): pl.pallas_call(kernel, out_shape=tuple((V(shape, kind) for shape, kind in...]
where the time goes in v2:
time: 86.2 us; the launch traced here: 86.1 us
  Pallas kernels  85.4 us (99%)
    pallas_call x1, Pallas kernels, per_device(): pl.pallas_call(kernel, out_shape=tuple((V(shape, kind) for shape, kind in...  84.2 us

profile of v2, /device:TPU:1, one launch (start us, length us, event | category | flops | bytes accessed | tf_op | source)
XLA Modules:
  0.0 86.1 jit_solution(723701525196074021)
XLA Ops:
  0.6 84.2 %shard_map.93 = (bf16[80,2048]{1,0:T(8,128)(2,1)S(1)}, bf16[432,1280]{1,0:T(8,128)(2,1)S(1)}, f32[8,2048]{1,0:T(8,128)S(1)}, bf16[32,2048]{1,0:T(8,128)(2,1)S(1)}) custom-call(s32[2,32]{1,0:T(2,128)} %bitcast.7, bf16[128,512]{1,0:T(8,128)(2,1)} %rin_ref.1, bf16[8,2048]{1,0:T(8,128)(2,1)} %bitcast.6, bf16[32,2048]{1,0:T(8,128)(2,1)} %grad_ref.1, ...), custom_call_target="tpu_custom_call" | custom-call | tf_op jit(solution)/shard_map/pallas_call | solution.py:448
  84.9 1.2 %shard_map.94 = (bf16[80,2048]{1,0:T(8,128)(2,1)}, bf16[432,1280]{1,0:T(8,128)(2,1)}, f32[8,2048]{1,0:T(8,128)}, bf16[32,2048]{1,0:T(8,128)(2,1)}) custom-call(bf16[80,2048]{1,0:T(8,128)(2,1)S(1)} %get-tuple-element.12.wg, bf16[432,1280]{1,0:T(8,128)(2,1)S(1)} %get-tuple-element.13.hg, f32[8,2048]{1,0:T(8,128)S(1)} %get-tuple-element.14.rg, ...), custom_call_target="tpu_custom_call" | custom-call | tf_op jit(solution)/shard_map/pallas_call | solution.py:491

commit v3 on v2

--- a/solution.py
+++ b/solution.py
@@ -29,6 +29,8 @@
 RP = 40
 RX = 112
 ROWS = NX * RX
+HALF = NZ // 2
+RH = RX // 2
 ZORDER = (6, 7, 5, 8, 4, 9, 3, 10, 2, 11, 1)
 PLUS, MINUS = 0, 1
 RS_SLOT = {}
@@ -61,7 +63,7 @@
     rp_send, rc_buf, ry_buf, rz_buf, rx_buf,
     wbuf, dbuf, rsbuf,
     load_sem,
-    zs_sem, zr_sem, xs_sem, xr_sem,
+    zs_sem, zr_sem, fs_sem, fr_sem, xs_sem, xr_sem,
     small_s, small_r,
     d_s, d_r, rs_s, rs_r,
 ):
@@ -70,7 +72,8 @@
     oc = 1 - c
     e_lo, e_hi = (z * NX) // 6, (z * NX + NX - 1) // 6
     middle = lax.rem(z, 3) == 1
-    sel_hi = lax.rem(z, 3) * (2 - lax.rem(z, 3))
+    third = lax.rem(z, 3)
+    sel_hi = third * (2 - third)
     zpeers = [lax.rem(z + k, NZ) for k in ZORDER]
     xpeers = [lax.rem(x + k, NX) for k in (2, 1, 3)]
     ypeers = [lax.rem(y + k, NY) for k in (4, 5, 3, 6, 2, 7, 1)]
@@ -142,20 +145,67 @@
         send(logit_buf.at[x], logit_buf.at[x], small_s.at[0], small_r.at[0], tensor=p)
 
     def z_send(q):
-        for p in zpeers:
-            lo, hi = (p * NX) // 6, (p * NX + NX - 1) // 6
-            send(chunk.at[q, lo], zbuf.at[0, q, z], zs_sem.at[0, q], zr_sem.at[0, q], expert=p)
-
-            @pl.when(lax.rem(p, 3) == 1)
+        for d in range(HALF - 1, 0, -1):
+            above, below = lax.rem(z + d, NZ), lax.rem(z + NZ - d, NZ)
+            ra, rb = lax.rem(above, 3), lax.rem(below, 3)
+
+            @pl.when(ra < 2)
             def _():
-                send(chunk.at[q, hi], zbuf.at[1, q, z], zs_sem.at[1, q], zr_sem.at[1, q], expert=p)
-
+                send(
+                    chunk.at[q, above // 3 * 2 + ra], zbuf.at[ra, q, d],
+                    zs_sem.at[q], zr_sem.at[ra, q], expert=above,
+                )
+
+            @pl.when(rb > 0)
+            def _():
+                send(
+                    chunk.at[q, below // 3 * 2 + rb - 1], zbuf.at[0, q, d],
+                    zs_sem.at[q], zr_sem.at[0, q], expert=below,
+                )
+
+    def z_own(q):
+        zbuf[0, q, 0] = chunk[q, e_lo]
+        zbuf[1, q, 0] = chunk[q, e_hi]
+
+    def z_forward(q):
+        near, far = pl.ds(0, HALF), pl.ds(HALF, HALF)
+        wait(zbuf.at[0, q, 1:HALF], zr_sem.at[0, q])
+        cls = third // 2
+        neighbour = jnp.where(third == 0, z + 1, z - 1)
+        send(
+            zbuf.at[0, q, near], zbuf.at[cls, q, far], fs_sem.at[0, q], fr_sem.at[cls, q], expert=neighbour
+        )
+
+        @pl.when(middle)
+        def _():
+            wait(zbuf.at[1, q, 1:HALF], zr_sem.at[1, q])
+            send(
+                zbuf.at[1, q, near], zbuf.at[0, q, far], fs_sem.at[1, q], fr_sem.at[0, q], expert=z + 1
+            )
+
+    z_own(0)
     z_send(0)
     for q in range(1, NQ):
         pack(q)
-    for q in range(NQ):
-        zbuf[0, q, z] = chunk[q, e_lo]
-        zbuf[1, q, z] = chunk[q, e_hi]
+        z_own(q)
+
+    rr, kk = iota((RH, HALF * RP), 0), iota((RH, HALF * RP), 1)
+    for b in range(LB):
+        relay_r[b] = onehot((kk == (rr // CAP) * RP + b * CAP + lax.rem(rr, CAP)) & (rr < HALF * CAP))
+    side = jnp.where((third == 0) | ((x // 2) * sel_hi == 1), -1, 1)
+
+    def place_of(row):
+        col, in_col = row // RX, lax.rem(row, RX)
+        in_half = lax.rem(in_col, RH)
+        dist, slot = in_half // CAP, lax.rem(in_half, CAP)
+        source = jnp.where(in_col < RH, z + side * dist, z - side - side * dist)
+        return col, lax.rem(source + 2 * NZ, NZ), slot, in_half < HALF * CAP
+
+    load(hid_hbm, hid, 0).wait()
+    col, source, slot, used = place_of(iota((ROWS, NX * NZ * CAP), 0))
+    perm = onehot((iota((ROWS, NX * NZ * CAP), 1) == (source * NX + col) * CAP + slot) & used)
+    hidp[...] = dot(perm, hid[...]).astype(BF16)
+    hidt[...] = hidp[...].T
 
     others = lambda ref, n: ref.at[0 : n - 1]
     wait(others(logit_buf, NX), small_r.at[0])
@@ -174,38 +224,29 @@
     for p in zpeers:
         send(pg_send, pg_buf.at[z], small_s.at[1], small_r.at[1], expert=p)
     z_send(1)
+
+    def z_relay(q, half):
+        if half:
+            wait(zbuf.at[0, q, HALF:NZ], fr_sem.at[0, q])
+
+            @pl.when(middle)
+            def _():
+                wait(zbuf.at[1, q, HALF:NZ], fr_sem.at[1, q])
+
+        for cls in range(2):
+            at = 0 if cls == 0 else sel_hi
+            rows = zbuf[at, q, half * HALF : (half + 1) * HALF].reshape(HALF * RP, 128)
+            for b in range(LB):
+                xsend[cls, q, half, :, b * 128 : (b + 1) * 128] = dot(relay_r[b], rows).astype(BF16)
+        for p in xpeers:
+            send(
+                xsend.at[p // 2, q, half], xbuf.at[q, x, half], xs_sem.at[q], xr_sem.at[q], tensor=p
+            )
+        xbuf[q, x, half] = xsend[x // 2, q, half]
+
+    z_forward(0)
+    z_relay(0, 0)
     z_send(2)
-    z_send(3)
-
-    rr, kk = iota((RX, NZ * RP), 0), iota((RX, NZ * RP), 1)
-    for b in range(LB):
-        relay_r[b] = onehot((kk == (rr // CAP) * RP + b * CAP + lax.rem(rr, CAP)) & (rr < NZ * CAP))
-
-    def z_relay(q):
-        wait(others(zbuf.at[0, q], NZ), zr_sem.at[0, q])
-
-        @pl.when(middle)
-        def _():
-            wait(others(zbuf.at[1, q], NZ), zr_sem.at[1, q])
-
-        for cls in range(2):
-            rows = zbuf[0 if cls == 0 else sel_hi, q].reshape(NZ * RP, 128)
-            for b in range(LB):
-                xsend[cls, q, :, b * 128 : (b + 1) * 128] = dot(relay_r[b], rows).astype(BF16)
-        for p in xpeers:
-            send(xsend.at[p // 2, q], xbuf.at[q, x], xs_sem.at[q], xr_sem.at[q], tensor=p)
-        xbuf[q, x] = xsend[x // 2, q]
-
-    load(hid_hbm, hid, 0).wait()
-    r1, m1 = iota((ROWS, NX * NZ * CAP), 0), iota((ROWS, NX * NZ * CAP), 1)
-    in_col = lax.rem(r1, RX)
-    perm = onehot(
-        (m1 == ((in_col // CAP) * NX + r1 // RX) * CAP + lax.rem(in_col, CAP)) & (in_col < NZ * CAP)
-    )
-    hidp[...] = dot(perm, hid[...]).astype(BF16)
-    hidt[...] = hidp[...].T
-
-    z_relay(0)
 
     wait(others(pg_buf, NZ), small_r.at[1])
     sub3 = iota((NZ, 8, 128), 1)
@@ -216,13 +257,19 @@
         send(pgx_send.at[p // 2], pgx_buf.at[x], small_s.at[2], small_r.at[2], tensor=p)
     pgx_buf[x] = pgx_send[x // 2]
 
-    z_relay(1)
-
-    rq, lq = iota((ROWS, 64), 0), iota((ROWS, 64), 1)
-    qc = lax.rem(rq, RX)
-    column_of = onehot((lq == (rq // RX) * 16 + qc // CAP) & (qc < NZ * CAP))
-    rw, lw = iota((ROWS, 128), 0), iota((ROWS, 128), 1)
-    own_slot = lw == lax.rem(lax.rem(rw, RX), CAP)
+    z_forward(1)
+    z_relay(1, 0)
+    z_relay(0, 1)
+    z_send(3)
+    z_forward(2)
+    z_relay(2, 0)
+    z_relay(1, 1)
+
+    col, source, slot, used = place_of(iota((ROWS, 64), 0))
+    column_of = onehot((iota((ROWS, 64), 1) == col * 16 + source) & used)
+    col, source, slot, used = place_of(iota((ROWS, 128), 0))
+    own_slot = iota((ROWS, 128), 1) == slot
+    own_row = (iota((ROWS, 128), 1) == source * CAP + slot) & used
 
     def make_gates():
         wait(others(pgx_buf, NX), small_r.at[2])
@@ -287,20 +334,23 @@
     make_gates()
     x_wait(0)
     weight_part(0)
+    z_forward(3)
+    z_relay(3, 0)
+    z_relay(2, 1)
     load(down_hbm, down, 1).wait()
     image_part(0)
-    z_relay(2)
     rs_first(0)
+    z_relay(3, 1)
     x_wait(1)
     weight_part(1)
     image_part(1)
-    z_relay(3)
     rs_step(0, 0)
     rs_first(1)
     x_wait(2)
+    weight_part(2)
     image_part(2)
-    weight_part(2)
     rs_step(0, 1)
+    rs_first(2)
     rs_step(1, 0)
     x_wait(3)
     image_part(3)
@@ -308,29 +358,30 @@
     slot_sum = jnp.sum(hidp[...].astype(F32) * image[...], axis=1, keepdims=True)
     rt, lt = iota((8, ROWS), 0), iota((8, ROWS), 1)
     back = jnp.where(rt == (x // 2) * sel_hi * NX + lt // RX, 1.0, 0.0)
-    own_row = (lw == lax.rem(rw, RX)) & (lw < NZ * CAP)
     gx_buf[x] = dot(back, jnp.where(own_row, slot_sum, 0.0), precision=HIGH)
     for p in xpeers:
         send(gx_buf.at[x], gx_buf.at[x], small_s.at[3], small_r.at[3], tensor=p)
 
     weight_part(3)
-    rs_first(2)
+    rs_step(0, 2)
 
     wait(others(gx_buf, NX), small_r.at[3])
     gz_buf[z] = gx_buf[0] + gx_buf[1] + gx_buf[2] + gx_buf[3]
     for p in zpeers:
         send(gz_buf.at[z], gz_buf.at[z], small_s.at[4], small_r.at[4], expert=p)
 
-    rs_step(0, 2)
+    rs_first(3)
     rs_step(1, 1)
-    rs_first(3)
+    rs_step(2, 0)
+    rs_step(0, 3)
 
     scaled = (gcol[:, 0:1] * image[...]).astype(BF16)
-    m2, r2 = iota((NX * NZ * CAP, ROWS), 0), iota((NX * NZ * CAP, ROWS), 1)
-    unperm = onehot(r2 == lax.rem(m2 // CAP, NX) * RX + (m2 // (CAP * NX)) * CAP + lax.rem(m2, CAP))
+    col, source, slot, used = place_of(iota((NX * NZ * CAP, ROWS), 1))
+    unperm = onehot((iota((NX * NZ * CAP, ROWS), 0) == (source * NX + col) * CAP + slot) & used)
     hg[...] = dot(unperm, scaled).astype(BF16)
 
-    rs_step(2, 0)
+    rs_step(3, 0)
+    rs_step(1, 2)
 
     wait(others(gz_buf, NZ), small_r.at[4])
     sums = []
@@ -353,23 +404,21 @@
     rp_send[1] = router[:, 256:512]
     send(rp_send.at[oc], rc_buf, small_s.at[5], small_r.at[5], dp_1=oc)
 
-    rs_step(0, 3)
-    rs_step(1, 2)
-
+    rs_step(2, 1)
     wait(rc_buf, small_r.at[5])
     pair = rp_send[c] + rc_buf[...]
     rz_buf[z] = pair
     for p in zpeers:
         send(rz_buf.at[z], rz_buf.at[z], small_s.at[6], small_r.at[6], expert=p)
 
-    rs_step(2, 1)
-    rs_step(3, 0)
+    rs_step(3, 1)
+    rs_step(1, 3)
+    rs_step(2, 2)
     tall[...] = jnp.concatenate([logit_grad] * 16, axis=0).T
     own_grad = tall[pl.ds(pl.multiple_of(x * TOK, TOK), TOK), 0:8]
     ig_ref[...] = dot(own_grad, rwt_ref[...].astype(F32), precision=HIGH).astype(BF16)
-    rs_step(1, 3)
-    rs_step(2, 2)
-
+    rs_step(3, 2)
+    rs_step(2, 3)
     wait(others(rz_buf, NZ), small_r.at[6])
     total = rz_buf[0]
     for p in range(1, NZ):
@@ -377,8 +426,7 @@
     ry_buf[y] = total
     for p in ypeers:
         send(ry_buf.at[y], ry_buf.at[y], small_s.at[7], small_r.at[7], dp_0=p)
-    rs_step(3, 1)
-    rs_step(2, 3)
+    rs_step(3, 3)
     wait(others(ry_buf, NY), small_r.at[7])
     total = ry_buf[0]
     for p in range(1, NY):
@@ -389,22 +437,21 @@
         for cc in (c, oc):
             send(rx_buf.at[here], rx_buf.at[here], small_s.at[8], small_r.at[8], tensor=p, dp_1=cc)
     send(rx_buf.at[here], rx_buf.at[here], small_s.at[8], small_r.at[8], dp_1=oc)
-    rs_step(3, 2)
-    rs_step(3, 3)
     wait(others(rx_buf, NX * NC), small_r.at[8])
     for i in range(NX * NC):
         rg_ref[:, i * 256 : (i + 1) * 256] = rx_buf[i]
 
     for q in range(NQ):
-        wait(others(zbuf.at[0, q], NZ), zs_sem.at[0, q])
+        wait(zbuf.at[0, q, 0:HALF], fs_sem.at[0, q])
 
         @pl.when(middle)
         def _():
-            wait(zbuf.at[1, q, 0:3], zs_sem.at[1, q])
+            wait(zbuf.at[0, q, 0 : NE - 2], zs_sem.at[q])
+            wait(zbuf.at[1, q, 0:HALF], fs_sem.at[1, q])
 
         @pl.when(jnp.logical_not(middle))
         def _():
-            wait(zbuf.at[1, q, 0:4], zs_sem.at[1, q])
+            wait(zbuf.at[0, q, 0 : NE - 1], zs_sem.at[q])
 
         wait(others(xbuf.at[q], NX), xs_sem.at[q])
         wait(dbuf.at[q], d_s.at[q])
@@ -457,13 +504,13 @@
             V((units, ROWS), BF16),
             V((ROWS, units), F32),
             V((ROWS, 128), F32),
-            V((LB, RX, NZ * RP), BF16),
+            V((LB, RH, HALF * RP), BF16),
             V((8, 128), I32),
             V((128, 128), F32),
             V((NQ, NE, RP, 128), BF16),
             V((2, NQ, NZ, RP, 128), BF16),
-            V((2, NQ, RX, QC), BF16),
-            V((NQ, NX, RX, QC), BF16),
+            V((2, NQ, 2, RH, QC), BF16),
+            V((NQ, NX, 2, RH, QC), BF16),
             V((NX, 16, 128), F32),
             V((8, 128), F32),
             V((NZ, 8, 128), F32),
@@ -480,7 +527,8 @@
             V((NQ, NY, 80, QC), BF16),
             V((NQ, NRS, 80, QC // 2), BF16),
             dma((2,)),
-            dma((2, NQ)), dma((2, NQ)), dma((NQ,)), dma((NQ,)),
+            dma((NQ,)), dma((2, NQ)), dma((2, NQ)), dma((2, NQ)),
+            dma((NQ,)), dma((NQ,)),
             dma((9,)), dma((9,)),
             dma((NQ,)), dma((NQ,)), dma((NQ,)), dma((NQ, NRS)),
         ],

time: 86.2 us -> 84.3 us (0.978)
  Pallas kernels: 85.4 us -> 83.5 us
    pallas_call x1, Pallas kernels: 84.2 us -> 82.3 us  [per_device(): pl.pallas_call(kernel, out_shape=tuple((V(shape, kind) for shape, kind in...]
where the time goes in v3:
time: 84.3 us; the launch traced here: 84.1 us
  Pallas kernels  83.5 us (99%)
    pallas_call x1, Pallas kernels, per_device(): pl.pallas_call(kernel, out_shape=tuple((V(shape, kind) for shape, kind in...  82.3 us

profile of v3, /device:TPU:1, one launch (start us, length us, event | category | flops | bytes accessed | tf_op | source)
XLA Modules:
  0.0 84.1 jit_solution(18321253812882591026)
XLA Ops:
  0.6 82.3 %shard_map.93 = (bf16[80,2048]{1,0:T(8,128)(2,1)S(1)}, bf16[432,1280]{1,0:T(8,128)(2,1)S(1)}, f32[8,2048]{1,0:T(8,128)S(1)}, bf16[32,2048]{1,0:T(8,128)(2,1)S(1)}) custom-call(s32[2,32]{1,0:T(2,128)} %bitcast.7, bf16[128,512]{1,0:T(8,128)(2,1)} %rin_ref.1, bf16[8,2048]{1,0:T(8,128)(2,1)} %bitcast.6, bf16[32,2048]{1,0:T(8,128)(2,1)} %grad_ref.1, ...), custom_call_target="tpu_custom_call" | custom-call | tf_op jit(solution)/shard_map/pallas_call | solution.py:495
  82.9 1.2 %shard_map.94 = (bf16[80,2048]{1,0:T(8,128)(2,1)}, bf16[432,1280]{1,0:T(8,128)(2,1)}, f32[8,2048]{1,0:T(8,128)}, bf16[32,2048]{1,0:T(8,128)(2,1)}) custom-call(bf16[80,2048]{1,0:T(8,128)(2,1)S(1)} %get-tuple-element.12.wg, bf16[432,1280]{1,0:T(8,128)(2,1)S(1)} %get-tuple-element.13.hg, f32[8,2048]{1,0:T(8,128)S(1)} %get-tuple-element.14.rg, ...), custom_call_target="tpu_custom_call" | custom-call | tf_op jit(solution)/shard_map/pallas_call | solution.py:539

commit v4 on v3

--- a/solution.py
+++ b/solution.py
@@ -247,6 +247,7 @@
     z_forward(0)
     z_relay(0, 0)
     z_send(2)
+    z_forward(1)
 
     wait(others(pg_buf, NZ), small_r.at[1])
     sub3 = iota((NZ, 8, 128), 1)
@@ -257,13 +258,12 @@
         send(pgx_send.at[p // 2], pgx_buf.at[x], small_s.at[2], small_r.at[2], tensor=p)
     pgx_buf[x] = pgx_send[x // 2]
 
-    z_forward(1)
+    z_relay(0, 1)
     z_relay(1, 0)
-    z_relay(0, 1)
     z_send(3)
     z_forward(2)
+    z_relay(1, 1)
     z_relay(2, 0)
-    z_relay(1, 1)
 
     col, source, slot, used = place_of(iota((ROWS, 64), 0))
     column_of = onehot((iota((ROWS, 64), 1) == col * 16 + source) & used)
@@ -335,23 +335,20 @@
     x_wait(0)
     weight_part(0)
     z_forward(3)
+    z_relay(2, 1)
     z_relay(3, 0)
-    z_relay(2, 1)
     load(down_hbm, down, 1).wait()
     image_part(0)
-    rs_first(0)
-    z_relay(3, 1)
     x_wait(1)
     weight_part(1)
+    z_relay(3, 1)
+    rs_first(0)
     image_part(1)
-    rs_step(0, 0)
     rs_first(1)
     x_wait(2)
     weight_part(2)
+    rs_step(0, 0)
     image_part(2)
-    rs_step(0, 1)
-    rs_first(2)
-    rs_step(1, 0)
     x_wait(3)
     image_part(3)
 
@@ -362,8 +359,10 @@
     for p in xpeers:
         send(gx_buf.at[x], gx_buf.at[x], small_s.at[3], small_r.at[3], tensor=p)
 
+    rs_step(0, 1)
     weight_part(3)
-    rs_step(0, 2)
+    rs_step(1, 0)
+    rs_first(2)
 
     wait(others(gx_buf, NX), small_r.at[3])
     gz_buf[z] = gx_buf[0] + gx_buf[1] + gx_buf[2] + gx_buf[3]
@@ -371,17 +370,13 @@
         send(gz_buf.at[z], gz_buf.at[z], small_s.at[4], small_r.at[4], expert=p)
 
     rs_first(3)
+    rs_step(0, 2)
     rs_step(1, 1)
-    rs_step(2, 0)
-    rs_step(0, 3)
 
     scaled = (gcol[:, 0:1] * image[...]).astype(BF16)
     col, source, slot, used = place_of(iota((NX * NZ * CAP, ROWS), 1))
     unperm = onehot((iota((NX * NZ * CAP, ROWS), 0) == (source * NX + col) * CAP + slot) & used)
     hg[...] = dot(unperm, scaled).astype(BF16)
-
-    rs_step(3, 0)
-    rs_step(1, 2)
 
     wait(others(gz_buf, NZ), small_r.at[4])
     sums = []
@@ -404,21 +399,22 @@
     rp_send[1] = router[:, 256:512]
     send(rp_send.at[oc], rc_buf, small_s.at[5], small_r.at[5], dp_1=oc)
 
-    rs_step(2, 1)
+    rs_step(2, 0)
     wait(rc_buf, small_r.at[5])
     pair = rp_send[c] + rc_buf[...]
     rz_buf[z] = pair
     for p in zpeers:
         send(rz_buf.at[z], rz_buf.at[z], small_s.at[6], small_r.at[6], expert=p)
 
-    rs_step(3, 1)
-    rs_step(1, 3)
-    rs_step(2, 2)
+    rs_step(3, 0)
+    rs_step(1, 2)
+    rs_step(0, 3)
     tall[...] = jnp.concatenate([logit_grad] * 16, axis=0).T
     own_grad = tall[pl.ds(pl.multiple_of(x * TOK, TOK), TOK), 0:8]
     ig_ref[...] = dot(own_grad, rwt_ref[...].astype(F32), precision=HIGH).astype(BF16)
-    rs_step(3, 2)
-    rs_step(2, 3)
+    rs_step(2, 1)
+    rs_step(3, 1)
+    rs_step(1, 3)
     wait(others(rz_buf, NZ), small_r.at[6])
     total = rz_buf[0]
     for p in range(1, NZ):
@@ -426,7 +422,8 @@
     ry_buf[y] = total
     for p in ypeers:
         send(ry_buf.at[y], ry_buf.at[y], small_s.at[7], small_r.at[7], dp_0=p)
-    rs_step(3, 3)
+    rs_step(2, 2)
+    rs_step(3, 2)
     wait(others(ry_buf, NY), small_r.at[7])
     total = ry_buf[0]
     for p in range(1, NY):
@@ -437,6 +434,8 @@
         for cc in (c, oc):
             send(rx_buf.at[here], rx_buf.at[here], small_s.at[8], small_r.at[8], tensor=p, dp_1=cc)
     send(rx_buf.at[here], rx_buf.at[here], small_s.at[8], small_r.at[8], dp_1=oc)
+    rs_step(2, 3)
+    rs_step(3, 3)
     wait(others(rx_buf, NX * NC), small_r.at[8])
     for i in range(NX * NC):
         rg_ref[:, i * 256 : (i + 1) * 256] = rx_buf[i]

time: 84.3 us -> 80.8 us (0.958)
  Pallas kernels: 83.5 us -> 80 us
    pallas_call x1, Pallas kernels: 82.3 us -> 78.8 us  [per_device(): pl.pallas_call(kernel, out_shape=tuple((V(shape, kind) for shape, kind in...]
where the time goes in v4:
time: 80.8 us; the launch traced here: 80.6 us
  Pallas kernels  80 us (99%)
    pallas_call x1, Pallas kernels, per_device(): pl.pallas_call(kernel, out_shape=tuple((V(shape, kind) for shape, kind in...  78.8 us

profile of v4, /device:TPU:1, one launch (start us, length us, event | category | flops | bytes accessed | tf_op | source)
XLA Modules:
  0.0 80.6 jit_solution(4785740249651347651)
XLA Ops:
  0.6 78.8 %shard_map.93 = (bf16[80,2048]{1,0:T(8,128)(2,1)S(1)}, bf16[432,1280]{1,0:T(8,128)(2,1)S(1)}, f32[8,2048]{1,0:T(8,128)S(1)}, bf16[32,2048]{1,0:T(8,128)(2,1)S(1)}) custom-call(s32[2,32]{1,0:T(2,128)} %bitcast.7, bf16[128,512]{1,0:T(8,128)(2,1)} %rin_ref.1, bf16[8,2048]{1,0:T(8,128)(2,1)} %bitcast.6, bf16[32,2048]{1,0:T(8,128)(2,1)} %grad_ref.1, ...), custom_call_target="tpu_custom_call" | custom-call | tf_op jit(solution)/shard_map/pallas_call | solution.py:494
  79.5 1.2 %shard_map.94 = (bf16[80,2048]{1,0:T(8,128)(2,1)}, bf16[432,1280]{1,0:T(8,128)(2,1)}, f32[8,2048]{1,0:T(8,128)}, bf16[32,2048]{1,0:T(8,128)(2,1)}) custom-call(bf16[80,2048]{1,0:T(8,128)(2,1)S(1)} %get-tuple-element.12.wg, bf16[432,1280]{1,0:T(8,128)(2,1)S(1)} %get-tuple-element.13.hg, f32[8,2048]{1,0:T(8,128)S(1)} %get-tuple-element.14.rg, ...), custom_call_target="tpu_custom_call" | custom-call | tf_op jit(solution)/shard_map/pallas_call | solution.py:538

commit v5 on v4

--- a/solution.py
+++ b/solution.py
@@ -185,7 +185,10 @@
 
     z_own(0)
     z_send(0)
-    for q in range(1, NQ):
+    pack(1)
+    z_own(1)
+    z_send(1)
+    for q in range(2, NQ):
         pack(q)
         z_own(q)
 
@@ -223,7 +226,7 @@
     pg_buf[z] = packed_gate
     for p in zpeers:
         send(pg_send, pg_buf.at[z], small_s.at[1], small_r.at[1], expert=p)
-    z_send(1)
+    z_send(2)
 
     def z_relay(q, half):
         if half:
@@ -246,8 +249,9 @@
 
     z_forward(0)
     z_relay(0, 0)
-    z_send(2)
     z_forward(1)
+    z_relay(1, 0)
+    z_send(3)
 
     wait(others(pg_buf, NZ), small_r.at[1])
     sub3 = iota((NZ, 8, 128), 1)
@@ -259,8 +263,6 @@
     pgx_buf[x] = pgx_send[x // 2]
 
     z_relay(0, 1)
-    z_relay(1, 0)
-    z_send(3)
     z_forward(2)
     z_relay(1, 1)
     z_relay(2, 0)
@@ -331,18 +333,18 @@
                 mine = dbuf[q, y, :, lo : lo + QC // 2].astype(F32)
                 wg_ref[:, q * QC + lo : q * QC + lo + QC // 2] = (mine + a + b).astype(BF16)
 
-    make_gates()
+    z_forward(3)
     x_wait(0)
-    weight_part(0)
-    z_forward(3)
+    load(down_hbm, down, 1).wait()
+    image_part(0)
     z_relay(2, 1)
     z_relay(3, 0)
-    load(down_hbm, down, 1).wait()
-    image_part(0)
+    make_gates()
+    weight_part(0)
+    z_relay(3, 1)
+    rs_first(0)
     x_wait(1)
     weight_part(1)
-    z_relay(3, 1)
-    rs_first(0)
     image_part(1)
     rs_first(1)
     x_wait(2)
@@ -414,7 +416,6 @@
     ig_ref[...] = dot(own_grad, rwt_ref[...].astype(F32), precision=HIGH).astype(BF16)
     rs_step(2, 1)
     rs_step(3, 1)
-    rs_step(1, 3)
     wait(others(rz_buf, NZ), small_r.at[6])
     total = rz_buf[0]
     for p in range(1, NZ):
@@ -434,6 +435,7 @@
         for cc in (c, oc):
             send(rx_buf.at[here], rx_buf.at[here], small_s.at[8], small_r.at[8], tensor=p, dp_1=cc)
     send(rx_buf.at[here], rx_buf.at[here], small_s.at[8], small_r.at[8], dp_1=oc)
+    rs_step(1, 3)
     rs_step(2, 3)
     rs_step(3, 3)
     wait(others(rx_buf, NX * NC), small_r.at[8])

time: 80.8 us -> 81.3 us (level)
  no operation moved by 1% of the time
where the time goes in v5:
time: 81.3 us; the launch traced here: 81.2 us
  Pallas kernels  80.5 us (99%)
    pallas_call x1, Pallas kernels, per_device(): pl.pallas_call(kernel, out_shape=tuple((V(shape, kind) for shape, kind in...  79.4 us

profile of v5, /device:TPU:1, one launch (start us, length us, event | category | flops | bytes accessed | tf_op | source)
XLA Modules:
  0.0 81.2 jit_solution(8660378971959779945)
XLA Ops:
  0.6 79.4 %shard_map.93 = (bf16[80,2048]{1,0:T(8,128)(2,1)S(1)}, bf16[432,1280]{1,0:T(8,128)(2,1)S(1)}, f32[8,2048]{1,0:T(8,128)S(1)}, bf16[32,2048]{1,0:T(8,128)(2,1)S(1)}) custom-call(s32[2,32]{1,0:T(2,128)} %bitcast.7, bf16[128,512]{1,0:T(8,128)(2,1)} %rin_ref.1, bf16[8,2048]{1,0:T(8,128)(2,1)} %bitcast.6, bf16[32,2048]{1,0:T(8,128)(2,1)} %grad_ref.1, ...), custom_call_target="tpu_custom_call" | custom-call | tf_op jit(solution)/shard_map/pallas_call | solution.py:496
  80.0 1.2 %shard_map.94 = (bf16[80,2048]{1,0:T(8,128)(2,1)}, bf16[432,1280]{1,0:T(8,128)(2,1)}, f32[8,2048]{1,0:T(8,128)}, bf16[32,2048]{1,0:T(8,128)(2,1)}) custom-call(bf16[80,2048]{1,0:T(8,128)(2,1)S(1)} %get-tuple-element.12.wg, bf16[432,1280]{1,0:T(8,128)(2,1)S(1)} %get-tuple-element.13.hg, f32[8,2048]{1,0:T(8,128)S(1)} %get-tuple-element.14.rg, ...), custom_call_target="tpu_custom_call" | custom-call | tf_op jit(solution)/shard_map/pallas_call | solution.py:540
